TPU v7x, 32 devices: a whole 2x2x4 slice. The times are simulated.
32 devices in a mesh: dp: 2 (over x), tp: 4 (over z), cp: 4 (over y, core).
Axes of the slice: x: 2, y: 2, z: 4, core: 2. Of those that a mesh axis runs over, the one named last changes fastest.
Arguments:
- hidden: bfloat16 [8, 1536, 6144], P('dp', 'cp'), parts along dimension 0
- alphas: float32 [2], replicated
- wq_attn: bfloat16 [6144, 8192], P(None, 'tp')
- wk_attn: bfloat16 [6144, 1024], P(None, 'tp')
- wv_attn: bfloat16 [6144, 1024], P(None, 'tp')
- wo_attn: bfloat16 [8192, 6144], P('tp')
- gain_attn: float32 [6144], replicated
- wq_lin: bfloat16 [6144, 8192], P(None, 'tp')
- wk_lin: bfloat16 [6144, 8192], P(None, 'tp')
- wv_lin: bfloat16 [6144, 8192], P(None, 'tp')
- wg_lin: bfloat16 [6144, 8192], P(None, 'tp')
- slopes: float32 [64], P('tp')
- gain_inner: float32 [8192], P('tp')
- wo_lin: bfloat16 [8192, 6144], P('tp')
- gain_lin: float32 [6144], replicated
Outputs:
- output: bfloat16 [8, 1536, 6144], P('dp', 'cp'), parts along dimension 0
There are 2 independent parts. A program takes and returns all parts, laid end to end along the dimension named above; an argument that names none is the same for every part.
All inputs are finite; a program needn't handle non-finite values.
Results may differ from a plain program's by a relative error of at most 0.012291.
Values are sent between devices in bfloat16 or wider.
A program may use at most 1 GiB of HBM per device.

v0:
```python
import math
import jax
import jax.numpy as jnp
from jax import lax
from jax.sharding import PartitionSpec as P

ROPE_BASE = 10000000.0
NORM_EPS = 1e-5


def rms_norm(values, gain_vec):
    return values * lax.rsqrt(jnp.mean(values * values, axis=-1, keepdims=True) + NORM_EPS) * gain_vec


def rotary(values, positions):
    rot_dims = values.shape[-1] // 2
    half = rot_dims // 2
    inv_freq = jnp.power(ROPE_BASE, -jnp.arange(half, dtype=jnp.float32) * 2.0 / rot_dims)
    angles = positions.astype(jnp.float32)[:, None] * inv_freq[None, :]
    cosine = jnp.cos(angles)[:, None, :]
    sine = jnp.sin(angles)[:, None, :]
    first = values[..., :half]
    second = values[..., half:rot_dims]
    return jnp.concatenate([first * cosine - second * sine, second * cosine + first * sine, values[..., rot_dims:]], axis=-1)


def attention_inputs(hidden, wq_attn, wk_attn, wv_attn, positions, head_dim):
    n_batch = hidden.shape[0]
    n_tok = hidden.shape[1]
    kv_heads = wk_attn.shape[1] // head_dim
    group = wq_attn.shape[1] // wk_attn.shape[1]
    q_proj = jnp.einsum('btm,mn->btn', hidden, wq_attn, preferred_element_type=jnp.float32)
    queries = rotary(q_proj.reshape(n_batch, n_tok, kv_heads * group, head_dim), positions).astype(jnp.bfloat16)
    k_proj = jnp.einsum('btm,mn->btn', hidden, wk_attn, preferred_element_type=jnp.float32)
    keys = rotary(k_proj.reshape(n_batch, n_tok, kv_heads, head_dim), positions).astype(jnp.bfloat16)
    values = jnp.einsum('btm,mn->btn', hidden, wv_attn, preferred_element_type=jnp.float32).astype(jnp.bfloat16)
    return queries.reshape(n_batch, n_tok, kv_heads, group, head_dim), keys, values.reshape(n_batch, n_tok, kv_heads, head_dim)


def softmax_init(queries):
    stats_shape = (queries.shape[0], queries.shape[2], queries.shape[3], queries.shape[1])
    return (jnp.full(stats_shape, -jnp.inf, jnp.float32), jnp.zeros(stats_shape, jnp.float32), jnp.zeros(stats_shape + (queries.shape[4],), jnp.float32))


def softmax_update(carry, queries, key_blk, value_blk, mask, scale):
    run_max, run_total, out_acc = carry
    scores = jnp.einsum('bqkgd,bskd->bkgqs', queries, key_blk, preferred_element_type=jnp.float32) * scale
    if mask is not None:
        scores = jnp.where(mask, scores, -jnp.inf)
    new_max = jnp.maximum(run_max, jnp.max(scores, axis=-1))
    factor = jnp.exp(run_max - new_max)
    prob_vals = jnp.exp(scores - new_max[..., None])
    run_total = run_total * factor + jnp.sum(prob_vals, axis=-1)
    out_acc = out_acc * factor[..., None] + jnp.einsum('bkgqs,bskd->bkgqd', prob_vals.astype(jnp.bfloat16), value_blk, preferred_element_type=jnp.float32)
    return new_max, run_total, out_acc


def attention_partial(carry, wo_attn):
    attn_vals = (carry[2] / carry[1][..., None]).astype(jnp.bfloat16)
    w_out = wo_attn.reshape(attn_vals.shape[1], attn_vals.shape[2], attn_vals.shape[4], wo_attn.shape[1])
    return jnp.einsum('bkgqd,kgdm->bqm', attn_vals, w_out, preferred_element_type=jnp.float32)


def lightning_inputs(mid_hidden, wq_lin, wk_lin, wv_lin, wg_lin, n_heads):
    n_batch = mid_hidden.shape[0]
    n_tok = mid_hidden.shape[1]

    def heads_of(weight):
        projected = jnp.einsum('btm,mn->btn', mid_hidden, weight, preferred_element_type=jnp.float32)
        return jax.nn.silu(projected).astype(jnp.bfloat16).reshape(n_batch, n_tok, n_heads, weight.shape[1] // n_heads)

    gate_vals = jax.nn.sigmoid(jnp.einsum('btm,mn->btn', mid_hidden, wg_lin, preferred_element_type=jnp.float32))
    return heads_of(wq_lin), heads_of(wk_lin), heads_of(wv_lin), gate_vals


def lightning_local(queries, keys, values, rates, tile):
    n_batch, n_tok, n_heads, head_dim = queries.shape
    n_tiles = n_tok // tile
    tiled_shape = (n_batch, n_tiles, tile, n_heads, head_dim)
    q_tiles = queries.reshape(tiled_shape)
    k_tiles = keys.reshape(tiled_shape)
    v_tiles = values.reshape(tiled_shape).astype(jnp.float32)
    offsets = jnp.arange(tile, dtype=jnp.float32)
    tok_gap = offsets[:, None] - offsets[None, :]
    intra_w = jnp.where(tok_gap >= 0, jnp.exp(-rates[:, None, None] * jnp.maximum(tok_gap, 0.0)), 0.0)
    scores = jnp.einsum('bnqhd,bnshd->bnhqs', q_tiles, k_tiles, preferred_element_type=jnp.float32) * intra_w
    inside = jnp.einsum('bnhqs,bnshd->bnqhd', scores, v_tiles)
    key_decay = jnp.exp(-rates[None, :] * (tile - 1.0 - offsets[:, None]))
    tile_states = jnp.einsum('bnshd,bnshe->bnhde', k_tiles * key_decay[:, :, None], v_tiles)
    tile_idx = jnp.arange(n_tiles, dtype=jnp.float32)
    tile_gap = tile_idx[:, None] - 1.0 - tile_idx[None, :]
    chain_w = jnp.where(tile_gap >= 0, jnp.exp(-rates[:, None, None] * tile * jnp.maximum(tile_gap, 0.0)), 0.0)
    entering = jnp.einsum('hnm,bmhde->bnhde', chain_w, tile_states)
    query_decay = jnp.exp(-rates[None, :] * (offsets[:, None] + 1.0))
    carried = jnp.einsum('bnqhd,bnhde->bnqhe', q_tiles.astype(jnp.float32), entering) * query_decay[:, :, None]
    end_w = jnp.exp(-rates[:, None] * tile * (n_tiles - 1.0 - tile_idx[None, :]))
    end_state = jnp.einsum('hn,bnhde->bhde', end_w, tile_states)
    return (inside + carried).reshape(queries.shape), end_state


def from_earlier(queries, prior_state, rates):
    steps = jnp.arange(queries.shape[1], dtype=jnp.float32) + 1.0
    weight = jnp.exp(-rates[None, :] * steps[:, None])
    return jnp.einsum('bthd,bhde->bthe', queries.astype(jnp.float32), prior_state) * weight[:, :, None]


def solution(mesh):
    cp_size = mesh.shape['cp']
    tp_size = mesh.shape['tp']
    shift = [(src, src + 1) for src in range(cp_size - 1)]
    tile = 128

    def body(hidden, alphas, wq_attn, wk_attn, wv_attn, wo_attn, gain_attn, wq_lin, wk_lin, wv_lin, wg_lin, slopes, gain_inner, wo_lin, gain_lin):
        n_heads = slopes.shape[0]
        head_dim = wq_lin.shape[1] // n_heads
        n_tok = hidden.shape[1]
        cp_idx = lax.axis_index('cp')
        positions = cp_idx * n_tok + jnp.arange(n_tok)
        queries, keys, values = attention_inputs(hidden, wq_attn, wk_attn, wv_attn, positions, head_dim)
        scale = 1.0 / math.sqrt(head_dim)
        tok_idx = jnp.arange(n_tok)
        causal = tok_idx[:, None] >= tok_idx[None, :]
        stats = softmax_update(softmax_init(queries), queries, keys, values, causal, scale)

        def kv_step(step_idx, state):
            run_stats, key_blk, value_blk = state
            key_blk, value_blk = lax.ppermute((key_blk, value_blk), 'cp', shift)
            run_stats = lax.cond(step_idx <= cp_idx, lambda prev: softmax_update(prev, queries, key_blk, value_blk, None, scale), lambda prev: prev, run_stats)
            return run_stats, key_blk, value_blk

        stats = lax.fori_loop(1, cp_size, kv_step, (stats, keys, values))[0]
        attn_sum = lax.psum(attention_partial(stats, wo_attn).astype(jnp.bfloat16), 'tp').astype(jnp.float32)
        mid_hidden = rms_norm(alphas[0] * hidden.astype(jnp.float32) + attn_sum, gain_attn).astype(jnp.bfloat16)

        lin_q, lin_k, lin_v, gate_vals = lightning_inputs(mid_hidden, wq_lin, wk_lin, wv_lin, wg_lin, n_heads)
        outputs, end_state = lightning_local(lin_q, lin_k, lin_v, slopes, tile)
        block_decay = jnp.exp(-slopes * n_tok)[None, :, None, None]

        def state_step(step_idx, state):
            incoming = lax.ppermute(state[1], 'cp', shift)
            return incoming, block_decay * incoming + end_state

        prior = lax.fori_loop(0, cp_size - 1, state_step, (jnp.zeros_like(end_state), end_state))[0]
        outputs = outputs + from_earlier(lin_q, prior, slopes)
        flat_out = outputs.reshape(gate_vals.shape)
        total_sq = lax.psum(jnp.sum(flat_out * flat_out, axis=-1, keepdims=True), 'tp')
        inner_vals = (flat_out * lax.rsqrt(total_sq / (flat_out.shape[-1] * tp_size) + NORM_EPS) * gain_inner * gate_vals).astype(jnp.bfloat16)
        lin_part = jnp.einsum('btn,nm->btm', inner_vals, wo_lin, preferred_element_type=jnp.float32)
        lin_sum = lax.psum(lin_part.astype(jnp.bfloat16), 'tp').astype(jnp.float32)
        return rms_norm(alphas[1] * mid_hidden.astype(jnp.float32) + lin_sum, gain_lin).astype(jnp.bfloat16)

    act_spec = P('dp', 'cp', None)
    rep_spec = P()
    col_spec = P(None, 'tp')
    row_spec = P('tp', None)
    vec_spec = P('tp')
    in_specs = (act_spec, rep_spec, col_spec, col_spec, col_spec, row_spec, rep_spec, col_spec, col_spec, col_spec, col_spec, vec_spec, vec_spec, row_spec, rep_spec)
    return jax.shard_map(body, mesh=mesh, in_specs=in_specs, out_specs=act_spec, check_vma=False)
```

profile of v0, /device:TPU:5, one launch (start us, length us, event | category | flops | bytes accessed | tf_op | source)
XLA Modules:
  0.0 2412.2 jit_solution(13868957344804399883)
XLA Ops:
  8.4 9.0 fusion.77
  23.2 48.7 %fusion.26 = f32[4,384,2048]{2,1,0:T(8,128)} fusion(bf16[4,384,6144]{2,1,0:T(8,128)(2,1)} %param.21, bf16[6144,2048]{1,0:T(8,128)(2,1)} %param.23), kind=kOutput, calls=%fused_computation.38 | convolution fusion | flops 38654705664 | bytes 56623104 | tf_op jit(solution)/shard_map/btm,mn->btn/dot_general | solution.py:32
  71.9 12.2 copy.89
  93.9 13.2 subtract_convert_fusion
  125.8 9.1 pad_maximum_fusion
  134.9 17.5 fusion.15
  152.4 16.9 fusion.14
  169.4 9.2 fusion.85
  179.8 20.7 broadcast_add_fusion
  200.5 227.4 %while.33 = (s32[]{:T(128)}, f32[4,2,8,384]{3,2,1,0:T(8,128)S(1)}, f32[4,2,8,384]{3,2,1,0:T(8,128)S(1)}, f32[4,2,8,384,128]{4,3,2,1,0:T(8,128)}, bf16[4,384,2,12...) while((s32[]{:T(128)}, f32[4,2,8,384]{3,2,1,0:T(8,128)S(1)}, ...), condition=%wide.region_7.8_spmd, body=%wide.region_2.7_spmd.sunk | while | flops 4913676288 | bytes 157286704 | solution.py:131
  207.0 58.2 %conditional.2 = ((f32[4,2,8,384]{3,2,1,0:T(8,128)S(1)}, f32[4,2,8,384]{3,2,1,0:T(8,128)S(1)}, f32[4,2,8,384,128]{4,3,2,1,0:T(8,128)})) conditional(s32[]{:T(128)} %convert_element_type.141, (f32[4,2,8,384]{3,2,1,0:T(8,128)S(1)}, f32[4,2,8,384]{3,2,1,0:T(8,128)S(1)}, f32[4,2,8,384,128]{4,3,2,1,0:T(8,128)}) %tuple.65, ...), branch_computations={%region_3.3_spmd, %region_4.6_spmd} | conditional | flops 4913676288 | bytes 147849248 | solution.py:128
  207.0 17.5 bitcast_reduce_fusion
  224.5 16.2 fusion.2
  240.8 24.4 %multiply_add_fusion = f32[4,2,8,384,128]{4,3,2,1,0:T(8,128)} fusion(f32[4,2,8,384,128]{4,3,2,1,0:T(8,128)} %get-tuple-element.182, f32[4,2,8,384]{3,2,1,0:T(8,128)S(1)} %get-tuple-element.250, f32[4,2,384,384,8]{3,2,4,1,0:T(8,128)} %get-tuple-element.252, f32[4,2,8,384]{3,2,1,0:T(8,128)S(1)} %max.14, bf16[4,384,2,128]{3,1,2,0:T(8,128)(2,1)S(1)} %get-tuple-element.183), kind=kOutput, calls=%fused_computation.8 | convolution fusion | flops 2450522112 | bytes 63897600 | tf_op jit(solution)/shard_map/while/body/eval_jaxpr/cond/branch_1_fun/bkgqs,bskd->bkgqd/dot_general | solution.py:54
  268.7 17.2 collective-permute-done
  287.8 58.2 %conditional.2 = ((f32[4,2,8,384]{3,2,1,0:T(8,128)S(1)}, f32[4,2,8,384]{3,2,1,0:T(8,128)S(1)}, f32[4,2,8,384,128]{4,3,2,1,0:T(8,128)})) conditional(s32[]{:T(128)} %convert_element_type.141, (f32[4,2,8,384]{3,2,1,0:T(8,128)S(1)}, f32[4,2,8,384]{3,2,1,0:T(8,128)S(1)}, f32[4,2,8,384,128]{4,3,2,1,0:T(8,128)}) %tuple.65, ...), branch_computations={%region_3.3_spmd, %region_4.6_spmd} | conditional | flops 4913676288 | bytes 147849248 | solution.py:128
  287.8 17.5 bitcast_reduce_fusion
  305.4 16.2 fusion.2
  321.7 24.4 %multiply_add_fusion = f32[4,2,8,384,128]{4,3,2,1,0:T(8,128)} fusion(f32[4,2,8,384,128]{4,3,2,1,0:T(8,128)} %get-tuple-element.182, f32[4,2,8,384]{3,2,1,0:T(8,128)S(1)} %get-tuple-element.250, f32[4,2,384,384,8]{3,2,4,1,0:T(8,128)} %get-tuple-element.252, f32[4,2,8,384]{3,2,1,0:T(8,128)S(1)} %max.14, bf16[4,384,2,128]{3,1,2,0:T(8,128)(2,1)S(1)} %get-tuple-element.183), kind=kOutput, calls=%fused_computation.8 | convolution fusion | flops 2450522112 | bytes 63897600 | tf_op jit(solution)/shard_map/while/body/eval_jaxpr/cond/branch_1_fun/bkgqs,bskd->bkgqd/dot_general | solution.py:54
  349.6 17.2 collective-permute-done
  368.7 58.2 %conditional.2 = ((f32[4,2,8,384]{3,2,1,0:T(8,128)S(1)}, f32[4,2,8,384]{3,2,1,0:T(8,128)S(1)}, f32[4,2,8,384,128]{4,3,2,1,0:T(8,128)})) conditional(s32[]{:T(128)} %convert_element_type.141, (f32[4,2,8,384]{3,2,1,0:T(8,128)S(1)}, f32[4,2,8,384]{3,2,1,0:T(8,128)S(1)}, f32[4,2,8,384,128]{4,3,2,1,0:T(8,128)}) %tuple.65, ...), branch_computations={%region_3.3_spmd, %region_4.6_spmd} | conditional | flops 4913676288 | bytes 147849248 | solution.py:128
  368.7 17.5 bitcast_reduce_fusion
  386.2 16.2 fusion.2
  402.5 24.4 %multiply_add_fusion = f32[4,2,8,384,128]{4,3,2,1,0:T(8,128)} fusion(f32[4,2,8,384,128]{4,3,2,1,0:T(8,128)} %get-tuple-element.182, f32[4,2,8,384]{3,2,1,0:T(8,128)S(1)} %get-tuple-element.250, f32[4,2,384,384,8]{3,2,4,1,0:T(8,128)} %get-tuple-element.252, f32[4,2,8,384]{3,2,1,0:T(8,128)S(1)} %max.14, bf16[4,384,2,128]{3,1,2,0:T(8,128)(2,1)S(1)} %get-tuple-element.183), kind=kOutput, calls=%fused_computation.8 | convolution fusion | flops 2450522112 | bytes 63897600 | tf_op jit(solution)/shard_map/while/body/eval_jaxpr/cond/branch_1_fun/bkgqs,bskd->bkgqd/dot_general | solution.py:54
  427.8 48.2 %bitcast_convert_fusion = bf16[4,384,6144]{2,1,0:T(8,128)(2,1)} fusion(bf16[2,8,128,6144,1]{3,2,1,0,4:T(8,128)(2,1)} %bitcast.217, f32[4,2,8,384,128]{4,3,2,1,0:T(8,128)} %get-tuple-element.204, f32[4,2,8,384]{3,2,1,0:T(8,128)S(1)} %get-tuple-element.205), kind=kOutput, calls=%fused_computation.16 | convolution fusion | flops 38670434304 | bytes 56721408 | tf_op jit(solution)/shard_map/bkgqd,kgdm->bqm/dot_general | solution.py:61
  482.4 620.8 %all-reduce.3.cloned.1.call-done = bf16[4,384,6144]{2,1,0:T(8,128)(2,1)} async-done(((bf16[4,384,6144]{2,1,0:T(8,128)(2,1)}), bf16[4,384,6144]{2,1,0:T(8,128)(2,1)}) %all-reduce.3.cloned.1.call-update) | async-done | bytes 18874384 | tf_op jit(solution)/shard_map/psum | solution.py:132
  1103.3 19.4 multiply_reduce_fusion.1
  1122.8 20.8 multiply_convert_fusion.1
  1143.5 49.5 %multiply_convert_fusion.3 = bf16[4,384,2048]{2,1,0:T(8,128)(2,1)} fusion(bf16[4,384,6144]{2,1,0:T(8,128)(2,1)} %multiply_convert_fusion.1, bf16[6144,2048]{1,0:T(8,128)(2,1)} %param.29), kind=kOutput, calls=%fused_computation.65 | convolution fusion | flops 38670434304 | bytes 50331648 | tf_op jit(solution)/shard_map/btm,mn->btn/dot_general | solution.py:69
  1200.8 9.1 copy.52
  1209.9 49.6 %multiply_convert_fusion.5 = bf16[4,384,2048]{2,1,0:T(8,128)(2,1)} fusion(bf16[4,384,6144]{2,1,0:T(8,128)(2,1)} %multiply_convert_fusion.1, bf16[6144,2048]{1,0:T(8,128)(2,1)} %param.30), kind=kOutput, calls=%fused_computation.67 | convolution fusion | flops 38670434304 | bytes 50331648 | tf_op jit(solution)/shard_map/btm,mn->btn/dot_general | solution.py:69
  1267.3 9.5 fusion.46
  1276.8 21.9 fusion.34
  1303.2 49.8 %multiply_convert_fusion.4 = bf16[4,384,2048]{2,1,0:T(8,128)(2,1)} fusion(bf16[4,384,6144]{2,1,0:T(8,128)(2,1)} %multiply_convert_fusion.1, bf16[6144,2048]{1,0:T(8,128)(2,1)} %param.28), kind=kOutput, calls=%fused_computation.66 | convolution fusion | flops 38670434304 | bytes 50331648 | tf_op jit(solution)/shard_map/btm,mn->btn/dot_general | solution.py:69
  1368.6 12.0 fusion.49
  1380.6 15.3 fusion.42
  1395.9 17.8 copy.55
  1413.7 12.7 copy.58
  1426.4 130.0 %while.34 = (s32[]{:T(128)}, f32[4,16,128,128]{3,2,1,0:T(8,128)}, f32[4,16,128,128]{3,2,1,0:T(8,128)}, f32[1,16,1,1]{1,3,2,0:T(1,128)S(1)}, f32[4,16,128,128]{3,2,1,0:T(8,128)}, /*index=5*/s32[]{:T(128)}) while((s32[]{:T(128)}, f32[4,16,128,128]{3,2,1,0:T(8,128)}, f32[4,16,128,128]{3,2,1,0:T(8,128)}, f32[1,16,1,1]{1,3,2,0:T(1,128)S(1)}, ...), condition=%wide.region_11.12_spmd, body=%wide.region_10.11_spmd.sunk | while | flops 2097154 | bytes 29360300 | solution.py:143
  1444.2 48.5 %collective-permute-done.2 = f32[4,16,128,128]{3,2,1,0:T(8,128)} collective-permute-done((f32[4,16,128,128]{3,2,1,0:T(8,128)}, f32[4,16,128,128]{3,2,1,0:T(8,128)}, u32[]{:S(2)}, u32[]{:S(2)}) %collective-permute-start.2) | collective-permute-done | bytes 4194336 | tf_op jit(solution)/shard_map/while/body/eval_jaxpr/ppermute | solution.py:140
  1500.8 48.5 %collective-permute-done.2 = f32[4,16,128,128]{3,2,1,0:T(8,128)} collective-permute-done((f32[4,16,128,128]{3,2,1,0:T(8,128)}, f32[4,16,128,128]{3,2,1,0:T(8,128)}, u32[]{:S(2)}, u32[]{:S(2)}) %collective-permute-start.2) | collective-permute-done | bytes 4194336 | tf_op jit(solution)/shard_map/while/body/eval_jaxpr/ppermute | solution.py:140
  1556.4 15.2 multiply_reduce_fusion.2
  1571.6 12.7 copy.84
  1592.0 48.6 %fusion.18 = f32[4,384,2048]{2,1,0:T(8,128)} fusion(bf16[4,384,6144]{2,1,0:T(8,128)(2,1)} %multiply_convert_fusion.1, bf16[6144,2048]{1,0:T(8,128)(2,1)} %param.31), kind=kOutput, calls=%fused_computation.30 | convolution fusion | flops 38654705664 | bytes 56623104 | tf_op jit(solution)/shard_map/btm,mn->btn/dot_general | solution.py:72
  1640.6 56.4 %fusion.38 = bf16[4,384,6144]{2,1,0:T(8,128)(2,1)} fusion(bf16[2048,6144]{1,0:T(8,128)(2,1)} %param.34, f32[4,384,2048]{2,1,0:T(8,128)} %fusion.18, f32[4,384,2048]{2,1,0:T(8,128)} %copy.84, f32[2048]{0:T(1024)S(1)} %copy-done.19, f32[4,384]{1,0:T(4,128)S(1)} %rsqrt_bitcast_fusion), kind=kOutput, calls=%fused_computation.49 | convolution fusion | flops 38686162944 | bytes 69220352 | tf_op jit(solution)/shard_map/btn,nm->btm/dot_general | solution.py:148
  1697.0 667.5 %all-reduce.5.cloned.1.call-done = bf16[4,384,6144]{2,1,0:T(8,128)(2,1)} async-done(((bf16[4,384,6144]{2,1,0:T(8,128)(2,1)}), bf16[4,384,6144]{2,1,0:T(8,128)(2,1)}) %all-reduce.5.cloned.1.call-update) | async-done | bytes 18874384 | tf_op jit(solution)/shard_map/psum | solution.py:149
  2364.6 19.2 multiply_reduce_fusion
  2383.9 21.0 multiply_convert_fusion
  (157 shorter events, 137.8 us)
Async XLA Ops:
  6.5 1.9 copy-start
  6.5 1096.7 %all-reduce.3.cloned.1.call-start = ((), (), s32[]{:S(2)}) async-start(), calls=%async_computation | async-start | bytes 37748736 | tf_op jit(solution)/shard_map/psum | solution.py:132
  107.1 11.6 slice-start.10
  114.3 4.3 slice-start.11
  114.3 9.8 slice-start.12
  118.7 4.8 copy-start.5
  118.7 5.5 slice-start.13
  123.0 2.8 copy-start.4
  152.4 17.0 copy-start.18
  200.7 4.4 collective-permute-start
  202.0 5.0 collective-permute-start.1
  266.1 19.8 collective-permute-start
  267.4 20.4 collective-permute-start.1
  347.0 19.8 collective-permute-start
  348.3 20.4 collective-permute-start.1
  476.0 0.7 copy-start.14
  476.0 1.3 copy-start.17
  476.1 1888.5 %all-reduce.5.cloned.1.call-start = ((), (), s32[]{:S(2)}) async-start(), calls=%async_computation.1 | async-start | bytes 37748736 | tf_op jit(solution)/shard_map/psum | solution.py:149
  477.9 644.8 %copy-start.15 = (f32[16]{0:T(128)}, f32[16]{0:T(128)S(1)}, u32[]{:S(2)}) copy-start(f32[16]{0:T(128)S(1)} %get-tuple-element.266) | copy-start | bytes 196
  1103.2 19.5 slice-start.5
  1103.2 19.5 slice-start.6
  1103.2 19.5 slice-start.7
  1103.2 19.5 slice-start.8
  1103.2 19.5 slice-start.9
  1103.3 19.5 copy-start.9
  1259.5 7.8 copy-start.8
  1267.3 9.5 copy-start.12
  1299.2 2.0 copy-start.2
  1353.0 8.0 slice-start.14
  1353.0 8.0 copy-start.13
  1353.0 8.0 copy-start.16
  1353.0 8.0 copy-start.20
  1353.1 8.0 slice-start.15
  1361.0 7.5 copy-start.3
  1368.6 12.0 copy-start.6
  1413.7 12.7 copy-start.11
  1426.4 130.0 %copy-start.7 = (f32[384,16]{0,1:T(8,128)S(1)}, f32[384,16]{0,1:T(8,128)}, u32[]{:S(2)}) copy-start(f32[384,16]{0,1:T(8,128)} %multiply_exponential_fusion) | copy-start | bytes 73732
  1426.4 9.7 collective-permute-start.2
  1442.9 49.8 %collective-permute-start.2 = (f32[4,16,128,128]{3,2,1,0:T(8,128)}, f32[4,16,128,128]{3,2,1,0:T(8,128)}, u32[]{:S(2)}, u32[]{:S(2)}) collective-permute-start(f32[4,16,128,128]{3,2,1,0:T(8,128)} %get-tuple-element.401), channel_id=1, source_target_pairs={{0,1},{1,2},{2,3},{4,5},{5,6},{6,7},{8,9},{9,10},{10,11},{12,13},{... | collective-permute-start | bytes 12582920 | tf_op jit(solution)/shard_map/while/body/eval_jaxpr/ppermute | solution.py:140
  1499.5 49.8 %collective-permute-start.2 = (f32[4,16,128,128]{3,2,1,0:T(8,128)}, f32[4,16,128,128]{3,2,1,0:T(8,128)}, u32[]{:S(2)}, u32[]{:S(2)}) collective-permute-start(f32[4,16,128,128]{3,2,1,0:T(8,128)} %get-tuple-element.401), channel_id=1, source_target_pairs={{0,1},{1,2},{2,3},{4,5},{5,6},{6,7},{8,9},{9,10},{10,11},{12,13},{... | collective-permute-start | bytes 12582920 | tf_op jit(solution)/shard_map/while/body/eval_jaxpr/ppermute | solution.py:140
  1592.0 48.6 %copy-start.19 = (f32[2048]{0:T(1024)S(1)}, f32[2048]{0:T(1024)}, u32[]{:S(2)}) copy-start(f32[2048]{0:T(1024)} %param.33) | copy-start | bytes 24580
  2364.6 19.3 slice-start
  2364.6 19.3 slice-start.1
  2364.6 19.3 slice-start.2
  2364.6 19.3 slice-start.3
  2364.6 19.3 slice-start.4
  2364.6 19.3 copy-start.10
  2383.9 21.0 copy-start.1
Sparse Core Ops, SparseCore 0:
  476.2 627.0 all-reduce.2
  1697.1 667.3 all-reduce.4
where the time goes:
time: 2420 us; the launch traced here: 2410 us
  waiting for transfers between devices  1440 us (60%)
  matrix products  614 us (25%)
  other arithmetic  196 us (8%)
  local copies, waits for them, and re-layouts  132 us (5%)
    psum x1, waiting for transfers between devices, body(): lin_sum = lax.psum(lin_part.astype(jnp.bfloat16), 'tp').astype(jnp.float32)  668 us
    psum x1, waiting for transfers between devices, body(): lax.psum(attention_partial(stats, wo_attn).astype(jnp.bfloat16), 'tp')  621 us
    dot_general x3, matrix products, heads_of(): jnp.einsum('btm,mn->btn', mid_hidden, weight, preferred_element_type=jnp....  149 us
    ppermute x3, waiting for transfers between devices, state_step(): incoming = lax.ppermute(state[1], 'cp', shift)  105 us
    dot_general x4, matrix products, softmax_update(): jnp.einsum('bkgqs,bskd->bkgqd', prob_vals.astype(jnp.bfloat16), value_blk...  93.7 us
    dot_general x4, matrix products, softmax_update(): jnp.einsum('bqkgd,bskd->bkgqs', queries, key_blk, preferred_element_type=...  70.1 us
    reduce_sum x4, other arithmetic, softmax_update(): run_total = run_total * factor + jnp.sum(prob_vals, axis=-1)  65.6 us
    dot_general x1, matrix products, body(): jnp.einsum('btn,nm->btm', inner_vals, wo_lin, preferred_element_type=jnp....  56.4 us
  transfers between devices with their start and end apart: 11, of which 11 were waited for; matrix products, arithmetic and copies ran while one was open for 0% of the time, Pallas kernels for 0%

commit v1 on v0

v1 whole, which is shorter than its diff:
```python
import functools
import math

import jax
import jax.numpy as jnp
from jax import lax
from jax.experimental import pallas as pl
from jax.experimental.pallas import tpu as pltpu
from jax.sharding import PartitionSpec as P

ROPE_BASE = 10000000.0
NORM_EPS = 1e-5
HEAD = 128
MESH = pl.DeviceIdType.MESH
F32 = jnp.float32
BF16 = jnp.bfloat16
ANY = pl.BlockSpec(memory_space=pl.ANY)
VMEM = pl.BlockSpec(memory_space=pltpu.VMEM)
SMEM = pl.BlockSpec(memory_space=pltpu.SMEM)

LEAD = 2
RING = 16
UNITS = 32
W_SLOTS = 3


def dot(lhs, rhs):
    return jnp.dot(lhs, rhs, preferred_element_type=F32)


def dot_t(lhs, rhs):
    return lax.dot_general(lhs, rhs, (((1,), (1,)), ((), ())), preferred_element_type=F32)


def rotary_tables(positions):
    rot = HEAD // 2
    half = rot // 2
    inv_freq = jnp.power(ROPE_BASE, -jnp.arange(half, dtype=F32) * 2.0 / rot)
    angles = positions.astype(F32)[:, None] * inv_freq[None, :]
    cosine, sine = jnp.cos(angles), jnp.sin(angles)
    n = positions.shape[0]
    same = jnp.concatenate([cosine, cosine, jnp.ones((n, HEAD - rot), F32)], axis=1)
    from_right = jnp.concatenate([-sine, jnp.zeros((n, HEAD - half), F32)], axis=1)
    from_left = jnp.concatenate([jnp.zeros((n, half), F32), sine, jnp.zeros((n, HEAD - rot), F32)], axis=1)
    return same, from_right, from_left


def attention_kernel(scale, n_heads, q_ref, k_ref, v_ref, same_ref, right_ref, left_ref, o_ref, acc, top, total):
    blk = lax.axis_index("cp")
    n_tok = q_ref.shape[0]
    quarter = HEAD // 4

    def head(h, carry):
        cols = pl.ds(pl.multiple_of(h * HEAD, HEAD), HEAD)
        raw = q_ref[:, cols]
        turned = raw * same_ref[...] + pltpu.roll(raw, HEAD - quarter, 1) * right_ref[...]
        query = (turned + pltpu.roll(raw, quarter, 1) * left_ref[...]).astype(BF16)

        scores = dot_t(query, k_ref[blk]) * scale
        rows = lax.broadcasted_iota(jnp.int32, scores.shape, 0)
        keys = lax.broadcasted_iota(jnp.int32, scores.shape, 1)
        scores = jnp.where(rows >= keys, scores, -jnp.inf)
        peak = jnp.max(scores, axis=-1, keepdims=True)
        probs = jnp.exp(scores - peak)
        top[...] = jnp.broadcast_to(peak, (n_tok, HEAD))
        total[...] = jnp.broadcast_to(jnp.sum(probs, axis=-1, keepdims=True), (n_tok, HEAD))
        acc[...] = dot(probs.astype(BF16), v_ref[blk])

        def earlier(j, inner):
            later_scores = dot_t(query, k_ref[j]) * scale
            old = top[:, 0:1]
            new = jnp.maximum(old, jnp.max(later_scores, axis=-1, keepdims=True))
            factor = jnp.exp(old - new)
            vals = jnp.exp(later_scores - new)
            top[...] = jnp.broadcast_to(new, (n_tok, HEAD))
            total[...] = total[...] * factor + jnp.sum(vals, axis=-1, keepdims=True)
            acc[...] = acc[...] * factor + dot(vals.astype(BF16), v_ref[j])
            return inner

        lax.fori_loop(0, blk, earlier, 0)
        o_ref[:, cols] = (acc[...] / total[...]).astype(BF16)
        return carry

    lax.fori_loop(0, n_heads, head, 0)


def attention(q_proj, kv_all, tables, n_tok):
    n_rows, width = q_proj.shape
    n_batch = n_rows // n_tok
    n_cp = kv_all.shape[0]
    kv_heads = kv_all.shape[3] // (2 * HEAD)
    per_kv = width // kv_heads
    table = pl.BlockSpec((n_tok, HEAD), lambda b, g: (0, 0))
    return pl.pallas_call(
        functools.partial(attention_kernel, 1.0 / math.sqrt(HEAD), per_kv // HEAD),
        out_shape=jax.ShapeDtypeStruct((n_rows, width), BF16),
        grid=(n_batch, kv_heads),
        in_specs=[
            pl.BlockSpec((n_tok, per_kv), lambda b, g: (b, g)),
            pl.BlockSpec((n_cp, None, n_tok, HEAD), lambda b, g: (0, b, 0, g)),
            pl.BlockSpec((n_cp, None, n_tok, HEAD), lambda b, g: (0, b, 0, kv_heads + g)),
            table,
            table,
            table,
        ],
        out_specs=pl.BlockSpec((n_tok, per_kv), lambda b, g: (b, g)),
        scratch_shapes=[pltpu.VMEM((n_tok, HEAD), F32)] * 3,
        compiler_params=pltpu.CompilerParams(vmem_limit_bytes=48 * 1024 * 1024),
        cost_estimate=pl.CostEstimate(flops=2 * n_rows * width * n_tok * 5, bytes_accessed=n_rows * width * 6, transcendentals=0),
    )(q_proj, kv_all, kv_all, *tables)


def fused_kernel(
    n_tp,
    n_cp,
    att,
    hid,
    wo_a,
    wk,
    wv,
    wq,
    wg,
    wo_l,
    gains,
    ginner,
    alphas,
    slopes,
    out,
    h1,
    part,
    summed,
    normed,
    w_buf,
    wo_buf,
    y_buf,
    kvq,
    gate,
    o_buf,
    state,
    state_in,
    res,
    wide,
    acc,
    sq_acc,
    row_inv,
    sq_send,
    sq_recv,
    reduce_send,
    reduce_recv,
    back_send,
    back_recv,
    res_sem,
    out_sem,
    w_sem,
    wo_sem,
    y_sem,
    state_send,
    state_recv,
    sq_send_sem,
    sq_recv_sem,
    credit,
):
    _, n_tok, model = part.shape
    width = y_buf.shape[1]
    n_heads = width // HEAD
    n_batch = att.shape[0] // n_tok
    half = n_tok // 2
    rows = res.shape[2]
    per_batch = half // rows
    per_group = per_batch // 4
    layer_pieces = n_batch * per_batch
    pieces = 2 * layer_pieces
    w_cols = w_buf.shape[2]
    wo_cols = wo_buf.shape[2]
    n_wo = model // wo_cols
    last = n_tp - 1
    trip = 2 * last * LEAD
    z = lax.axis_index("tp")
    c = lax.axis_index("cp")

    barrier = pltpu.get_barrier_semaphore()
    for k in range(1, n_tp):
        pl.semaphore_signal(barrier, inc=1, device_id={"tp": lax.rem(z + k, n_tp)}, device_id_type=MESH)

    @pl.when(c > 0)
    def _():
        pl.semaphore_signal(barrier, inc=1, device_id={"cp": c - 1}, device_id_type=MESH)

    @pl.when(c < n_cp - 1)
    def _():
        pl.semaphore_signal(barrier, inc=1, device_id={"cp": c + 1}, device_id_type=MESH)

    inner = (c > 0) & (c < n_cp - 1)

    @pl.when(inner)
    def _():
        pl.semaphore_wait(barrier, n_tp + 1)

    @pl.when(jnp.logical_not(inner))
    def _():
        pl.semaphore_wait(barrier, n_tp)

    def row_of(g, f):
        return pl.multiple_of(f * half + lax.rem(g, per_batch) * rows, rows)

    def view(ref, g, f):
        return ref.at[lax.rem(lax.div(g, per_batch), 2), pl.ds(row_of(g, f), rows), :]

    def place(f):
        return (z, z + 1, z - 1) if f == 0 else (last - z, z - 1, z + 1)

    def forward(g, f):
        slot = lax.rem(g, RING)
        return pltpu.make_async_remote_copy(
            src_ref=view(part, g, f),
            dst_ref=view(summed, g, f),
            send_sem=reduce_send.at[f, slot],
            recv_sem=reduce_recv.at[f, slot],
            device_id={"tp": place(f)[1]},
            device_id_type=MESH,
        )

    def backward(g, f):
        slot = lax.rem(g, RING)
        return pltpu.make_async_remote_copy(
            src_ref=view(summed, g, f),
            dst_ref=view(summed, g, f),
            send_sem=back_send.at[f, slot],
            recv_sem=back_recv.at[f, slot],
            device_id={"tp": place(f)[2]},
            device_id_type=MESH,
        )

    def hbm_rows(ref, g, f):
        batch = lax.rem(lax.div(g, per_batch), n_batch)
        return ref.at[pl.ds(pl.multiple_of(batch * n_tok + row_of(g, f), rows), rows), :]

    def res_copy(g, f, ref):
        slot = lax.rem(g, 4)
        return pltpu.make_async_copy(hbm_rows(ref, g, f), res.at[f, slot], res_sem.at[f, slot])

    def out_copy(g, f, ref):
        return pltpu.make_async_copy(view(normed, g, f), hbm_rows(ref, g, f), out_sem.at[f, lax.rem(g, 4)])

    def norm_rows(g, f):
        layer = (g >= layer_pieces).astype(jnp.int32)
        slot = lax.rem(g, 4)
        at = lax.rem(lax.div(g, per_batch), 2)
        span = pl.ds(row_of(g, f), rows)
        alpha = alphas[layer]
        n_chunk = model // wo_cols

        def first(i, sq):
            cols = pl.ds(pl.multiple_of(i * wo_cols, wo_cols), wo_cols)
            vals = alpha * res[f, slot, :, cols].astype(F32) + summed[at, span, cols].astype(F32)
            wide[:, cols] = vals
            return sq + vals * vals

        sq = lax.fori_loop(0, n_chunk, first, jnp.zeros((rows, wo_cols), F32))
        scale = lax.rsqrt(jnp.sum(sq, axis=-1, keepdims=True) / model + NORM_EPS)

        def second(i, carry):
            cols = pl.ds(pl.multiple_of(i * wo_cols, wo_cols), wo_cols)
            normed[at, span, cols] = (wide[:, cols] * scale * gains[layer, :, cols]).astype(BF16)
            return carry

        lax.fori_loop(0, n_chunk, second, 0)

    def known(g):
        return (g >= 0) & (g < pieces)

    def service(step):
        ahead = step + 3 - trip
        for f in range(2):

            @pl.when((ahead >= 0) & (ahead < layer_pieces))
            def _():
                res_copy(ahead, f, hid).start()

            @pl.when((ahead >= layer_pieces) & (ahead < pieces))
            def _():
                res_copy(ahead, f, h1).start()

        for f in range(2):
            pos = place(f)[0]
            g = step - LEAD * pos

            @pl.when(known(g) & (pos > 0))
            def _():
                forward(g, f).wait_recv()

            @pl.when(known(g) & (pos > 0) & (pos < last))
            def _():
                at = lax.rem(lax.div(g, per_batch), 2)
                span = pl.ds(row_of(g, f), rows)
                part[at, span, :] = part[at, span, :] + summed[at, span, :]

            @pl.when(known(g) & (pos == last))
            def _():
                at = lax.rem(lax.div(g, per_batch), 2)
                span = pl.ds(row_of(g, f), rows)
                summed[at, span, :] = part[at, span, :] + summed[at, span, :]

        for f in range(2):
            pos = place(f)[0]
            g = step - LEAD * pos

            @pl.when(known(g) & (pos < last))
            def _():
                forward(g, f).start()

            @pl.when(known(g) & (pos == last))
            def _():
                backward(g, f).start()

        for f in range(2):
            pos = place(f)[0]
            g = step - LEAD * (2 * last - pos)

            @pl.when(known(g) & (pos < last))
            def _():
                backward(g, f).wait_recv()

            @pl.when(known(g) & (pos < last) & (pos > 0))
            def _():
                backward(g, f).start()

        for f in range(2):
            pos = place(f)[0]
            sent = step - (LEAD * (last - 1) + 3)

            @pl.when(known(sent) & (pos < last))
            def _():
                forward(sent, f).wait_send()

        done = step - trip

        @pl.when(known(done))
        def _():
            for f in range(2):
                pos = place(f)[0]

                @pl.when(pos > 0)
                def _():
                    backward(done, f).wait_send()

                @pl.when(done < layer_pieces)
                def _():
                    res_copy(done, f, hid).wait()

                @pl.when(done >= layer_pieces)
                def _():
                    res_copy(done, f, h1).wait()

                @pl.when(done >= 4)
                def _():
                    out_copy(done - 4, f, out).wait()

                norm_rows(done, f)

                @pl.when(done < layer_pieces)
                def _():
                    out_copy(done, f, h1).start()

                @pl.when(done >= layer_pieces)
                def _():
                    out_copy(done, f, out).start()

    projections = (wk, wv, wq, wg)

    def w_copy(which, tile, slot):
        cols = pl.ds(pl.multiple_of(tile * w_cols, w_cols), w_cols)
        return pltpu.make_async_copy(projections[which].at[:, cols], w_buf.at[slot], w_sem.at[slot])

    def wo_copy(weight, tile):
        cols = pl.ds(pl.multiple_of(tile * wo_cols, wo_cols), wo_cols)
        slot = lax.rem(tile, 2)
        return pltpu.make_async_copy(weight.at[:, cols], wo_buf.at[slot], wo_sem.at[slot])

    def has_projection(phase):
        return (phase >= 2) & (phase < 2 + n_batch)

    def project(unit, phase, which, tile):
        slot = lax.rem(unit, W_SLOTS)
        w_copy(0, tile, slot).wait()
        at = lax.rem(phase, 2)
        depth = model // 6
        acc[:, 0:w_cols] = jnp.zeros((n_tok, w_cols), F32)

        def chunk(i, carry):
            ks = pl.ds(pl.multiple_of(i * depth, depth), depth)
            acc[:, 0:w_cols] += dot(normed[at, :, ks], w_buf[slot, ks, :])
            return carry

        lax.fori_loop(0, 6, chunk, 0)
        cols = pl.ds(pl.multiple_of(tile * w_cols, w_cols), w_cols)
        vals = acc[:, 0:w_cols]
        soft = jax.nn.sigmoid(vals)

        @pl.when(which < 3)
        def _():
            kvq[which, :, cols] = (vals * soft).astype(BF16)

        @pl.when(which == 3)
        def _():
            gate[:, cols] = soft

    def out_project(phase, tile):
        wo_copy(wo_a, tile).wait()
        slot = lax.rem(tile, 2)
        cols = pl.ds(pl.multiple_of(tile * wo_cols, wo_cols), wo_cols)
        at = lax.rem(phase + 1, 2)
        part[at, :, cols] = dot(y_buf[...], wo_buf[slot]).astype(BF16)

    def state_copy():
        return pltpu.make_async_remote_copy(
            src_ref=state,
            dst_ref=state_in,
            send_sem=state_send,
            recv_sem=state_recv,
            device_id={"cp": c + 1},
            device_id_type=MESH,
        )

    def local_lightning():
        def head(h, carry):
            cols = pl.ds(pl.multiple_of(h * HEAD, HEAD), HEAD)
            rate = slopes[h]
            key, value, query = kvq[0, :, cols], kvq[1, :, cols], kvq[2, :, cols]
            scores = dot_t(query, key)
            gap = lax.broadcasted_iota(jnp.int32, scores.shape, 0) - lax.broadcasted_iota(jnp.int32, scores.shape, 1)
            decay = jnp.where(gap >= 0, jnp.exp(-rate * gap.astype(F32)), 0.0)
            o_buf[:, cols] = dot((scores * decay).astype(BF16), value)
            to_end = (n_tok - 1 - lax.broadcasted_iota(jnp.int32, (n_tok, HEAD), 0)).astype(F32)
            faded = key.astype(F32) * jnp.exp(-rate * to_end)
            state[h] = dot(faded.T.astype(BF16), value)
            return carry

        lax.fori_loop(0, n_heads, head, 0)

    def add_incoming():
        def head(h, carry):
            state[h] = state_in[h] * jnp.exp(jnp.zeros((HEAD, HEAD), F32) - slopes[h] * n_tok) + state[h]
            return carry

        lax.fori_loop(0, n_heads, head, 0)

    def send_state(batch):
        @pl.when(batch > 0)
        def _():
            pl.semaphore_wait(credit, 1)

        state_copy().start()

    def sq_copy(batch, k):
        peer = lax.rem(z + k, n_tp)
        return pltpu.make_async_remote_copy(
            src_ref=sq_send,
            dst_ref=sq_recv.at[batch, z],
            send_sem=sq_send_sem.at[k],
            recv_sem=sq_recv_sem.at[batch, z],
            device_id={"tp": peer},
            device_id_type=MESH,
        )

    def sq_arrival(batch, k):
        source = lax.rem(z + n_tp - k, n_tp)
        return pltpu.make_async_remote_copy(
            src_ref=sq_send,
            dst_ref=sq_recv.at[batch, source],
            send_sem=sq_send_sem.at[k],
            recv_sem=sq_recv_sem.at[batch, source],
            device_id={"tp": source},
            device_id_type=MESH,
        )

    def add_earlier(batch):
        @pl.when(c == n_cp - 1)
        def _():
            state_copy().wait_recv()

        @pl.when(c < n_cp - 1)
        def _():
            state_copy().wait_send()

        sq_acc[...] = jnp.zeros_like(sq_acc)

        def head(h, carry):
            cols = pl.ds(pl.multiple_of(h * HEAD, HEAD), HEAD)

            @pl.when(c > 0)
            def _():
                steps = (lax.broadcasted_iota(jnp.int32, (n_tok, HEAD), 0) + 1).astype(F32)
                prior = dot(kvq[2, :, cols], state_in[h].astype(BF16))
                o_buf[:, cols] += prior * jnp.exp(-slopes[h] * steps)

            vals = o_buf[:, cols]
            sq_acc[...] += vals * vals
            return carry

        lax.fori_loop(0, n_heads, head, 0)

        @pl.when((c > 0) & (batch < n_batch - 1))
        def _():
            pl.semaphore_signal(credit, inc=1, device_id={"cp": c - 1}, device_id_type=MESH)

        row_sq = jnp.broadcast_to(jnp.sum(sq_acc[...], axis=-1, keepdims=True), (n_tok, HEAD))
        sq_send[...] = row_sq.T[0:8, :]
        sq_recv[batch, z] = sq_send[...]
        for k in range(1, n_tp):
            sq_copy(batch, k).start()

    def finish_lightning(batch):
        for k in range(1, n_tp):
            sq_arrival(batch, k).wait_recv()
        for k in range(1, n_tp):
            sq_copy(batch, k).wait_send()
        total = sq_recv[batch, 0]
        for k in range(1, n_tp):
            total = total + sq_recv[batch, k]
        tall = jnp.broadcast_to(total[0:1, :], (HEAD, n_tok)).T
        row_inv[...] = lax.rsqrt(tall / (width * n_tp) + NORM_EPS)

        def head(h, carry):
            cols = pl.ds(pl.multiple_of(h * HEAD, HEAD), HEAD)
            y_buf[:, cols] = (o_buf[:, cols] * row_inv[...] * ginner[h] * gate[:, cols]).astype(BF16)
            return carry

        lax.fori_loop(0, n_heads, head, 0)

    def unit_body(unit, carry):
        phase = lax.div(unit, UNITS) - 1
        r = lax.rem(unit, UNITS)
        which = lax.div(r, 8)
        tile = lax.rem(r, 8)
        first_layer = phase < n_batch - 1
        second_layer = (phase >= 3) & (phase < 3 + n_batch)
        projects = has_projection(phase)

        @pl.when(lax.rem(tile, 3) == 0)
        def _():
            part_of = lax.div(tile, 3)

            def one(i, inner):
                service(phase * per_batch + which * per_group + part_of * (per_group // 3) + i)
                return inner

            if per_group == 3:
                one(0, 0)
            else:
                lax.fori_loop(0, per_group // 3, one, 0)

        @pl.when((r == 8) & first_layer)
        def _():
            batch_rows = pl.ds(pl.multiple_of((phase + 1) * n_tok, n_tok), n_tok)
            pltpu.make_async_copy(att.at[batch_rows, :], y_buf, y_sem).start()

        for i in range(2):

            @pl.when((r == 8 + i) & first_layer)
            def _():
                wo_copy(wo_a, i).start()

            @pl.when((r == 8 + i) & second_layer)
            def _():
                wo_copy(wo_l, i).start()

        @pl.when((r == 4) & second_layer & (c == 2))
        def _():
            state_copy().wait_recv()
            add_incoming()
            send_state(phase - 3)

        @pl.when((r == 12) & second_layer)
        def _():
            add_earlier(phase - 3)

        @pl.when((r == 16) & second_layer)
        def _():
            finish_lightning(phase - 3)

        @pl.when((r == 16) & first_layer)
        def _():
            pltpu.make_async_copy(att.at[pl.ds(0, n_tok), :], y_buf, y_sem).wait()

        wo_tile = r - 16

        @pl.when((wo_tile >= 0) & (wo_tile < n_wo) & (first_layer | second_layer))
        def _():
            out_project(phase, wo_tile)

            @pl.when((wo_tile < n_wo - 2) & first_layer)
            def _():
                wo_copy(wo_a, wo_tile + 2).start()

            @pl.when((wo_tile < n_wo - 2) & second_layer)
            def _():
                wo_copy(wo_l, wo_tile + 2).start()

        @pl.when(projects)
        def _():
            project(unit, phase, which, tile)

        coming = unit + W_SLOTS
        coming_r = lax.rem(coming, UNITS)

        @pl.when(has_projection(lax.div(coming, UNITS) - 1))
        def _():
            for k in range(4):

                @pl.when(lax.div(coming_r, 8) == k)
                def _():
                    w_copy(k, lax.rem(coming_r, 8), lax.rem(coming, W_SLOTS)).start()

        @pl.when((r == 23) & projects)
        def _():
            local_lightning()

            @pl.when(c == 0)
            def _():
                send_state(phase - 2)

        @pl.when((r == 28) & projects & (c == 1))
        def _():
            state_copy().wait_recv()
            add_incoming()
            send_state(phase - 2)

        return carry

    n_phases = 2 * n_batch + 2
    lax.fori_loop(0, n_phases * UNITS, unit_body, 0)
    for f in range(2):
        for k in range(4):
            out_copy(pieces - 4 + k, f, out).wait()


def fused_layers(att, hid, weights, gains, ginner, alphas, slopes, n_tok, n_tp, n_cp):
    wo_a, wk, wv, wq, wg, wo_l = weights
    n_rows, width = att.shape
    model = hid.shape[1]
    n_batch = n_rows // n_tok
    n_heads = width // HEAD
    rows = n_tok // 24
    w_cols = width // 8
    wo_cols = model // 12
    vmem, dma = pltpu.VMEM, pltpu.SemaphoreType.DMA
    scratch = [
        vmem((2, n_tok, model), BF16),
        vmem((2, n_tok, model), BF16),
        vmem((2, n_tok, model), BF16),
        vmem((W_SLOTS, model, w_cols), BF16),
        vmem((2, width, wo_cols), BF16),
        vmem((n_tok, width), BF16),
        vmem((3, n_tok, width), BF16),
        vmem((n_tok, width), F32),
        vmem((n_tok, width), F32),
        vmem((n_heads, HEAD, HEAD), F32),
        vmem((n_heads, HEAD, HEAD), F32),
        vmem((2, 4, rows, model), BF16),
        vmem((rows, model), F32),
        vmem((n_tok, max(w_cols, HEAD)), F32),
        vmem((n_tok, HEAD), F32),
        vmem((n_tok, HEAD), F32),
        vmem((8, n_tok), F32),
        vmem((n_batch, n_tp, 8, n_tok), F32),
        dma((2, RING)),
        dma((2, RING)),
        dma((2, RING)),
        dma((2, RING)),
        dma((2, 4)),
        dma((2, 4)),
        dma((W_SLOTS,)),
        dma((2,)),
        dma,
        dma,
        dma,
        dma((n_tp,)),
        dma((n_batch, n_tp)),
        pltpu.SemaphoreType.REGULAR,
    ]
    flops = 2 * n_rows * model * width * 6
    return pl.pallas_call(
        functools.partial(fused_kernel, n_tp, n_cp),
        out_shape=[jax.ShapeDtypeStruct((n_rows, model), BF16)] * 2,
        in_specs=[ANY] * 8 + [VMEM] * 2 + [SMEM] * 2,
        out_specs=[ANY] * 2,
        scratch_shapes=scratch,
        compiler_params=pltpu.CompilerParams(collective_id=0, has_side_effects=True, vmem_limit_bytes=67043328),
        cost_estimate=pl.CostEstimate(flops=flops, bytes_accessed=12 * n_rows * model, transcendentals=0),
    )(att, hid, wo_a, wk, wv, wq, wg, wo_l, gains, ginner, alphas, slopes)


def solution(mesh):
    n_tp, n_cp = mesh.shape["tp"], mesh.shape["cp"]

    def body(hidden, alphas, wq_attn, wk_attn, wv_attn, wo_attn, gain_attn, wq_lin, wk_lin, wv_lin, wg_lin, slopes, gain_inner, wo_lin, gain_lin):
        n_batch, n_tok, model = hidden.shape
        flat = hidden.reshape(n_batch * n_tok, model)
        kv_width = wk_attn.shape[1]
        positions = lax.axis_index("cp") * n_tok + jnp.arange(n_tok)
        tables = rotary_tables(positions)

        k_proj = dot(flat, wk_attn).reshape(n_batch, n_tok, kv_width // HEAD, HEAD)
        same, from_right, from_left = (t[None, :, None, :] for t in tables)
        quarter = HEAD // 4
        keys = k_proj * same + jnp.roll(k_proj, -quarter, axis=-1) * from_right + jnp.roll(k_proj, quarter, axis=-1) * from_left
        keys = keys.astype(BF16).reshape(n_batch, n_tok, kv_width)
        values = dot(flat, wv_attn).astype(BF16).reshape(n_batch, n_tok, kv_width)
        kv_all = lax.all_gather(jnp.concatenate([keys, values], axis=-1), "cp")

        q_proj = dot(flat, wq_attn)
        att = attention(q_proj, kv_all, tables, n_tok)
        gains = jnp.stack([gain_attn, gain_lin])[:, None, :]
        weights = (wo_attn, wk_lin, wv_lin, wq_lin, wg_lin, wo_lin)
        out, _ = fused_layers(att, flat, weights, gains, gain_inner.reshape(-1, 1, HEAD), alphas, slopes, n_tok, n_tp, n_cp)
        return out.reshape(hidden.shape)

    act_spec = P("dp", "cp", None)
    rep_spec = P()
    col_spec = P(None, "tp")
    row_spec = P("tp", None)
    vec_spec = P("tp")
    in_specs = (act_spec, rep_spec, col_spec, col_spec, col_spec, row_spec, rep_spec, col_spec, col_spec, col_spec, col_spec, vec_spec, vec_spec, row_spec, rep_spec)
    return jax.shard_map(body, mesh=mesh, in_specs=in_specs, out_specs=act_spec, check_vma=False)
```

time: 2420 us -> 1210 us (0.50)
  waiting for transfers between devices: 1440 us -> 0.02 us
  Pallas kernels: 0 us -> 1090 us
  matrix products: 614 us -> 68.3 us
  other arithmetic: 196 us -> 6.97 us
  local copies, waits for them, and re-layouts: 132 us -> 27.8 us
    psum x2 -> x0, waiting for transfers between devices: 1290 us -> none  [the longest x1 668 us: body(): lin_sum = lax.psum(lin_part.astype(jnp.bfloat16), 'tp').astype(jnp.float32)]
    pallas_call x0 -> x2, Pallas kernels: none -> 1090 us  [the longest x1 913 us: fused_layers(): pl.pallas_call(functools.partial(fused_kernel, n_tp, n_cp), out_shape=[ja...]
    dot_general x23 -> x3, matrix products: 614 us -> 68.3 us  [dot(): return jnp.dot(lhs, rhs, preferred_element_type=F32)]
    ppermute x9 -> x0, waiting for transfers between devices: 147 us -> none  [the longest x3 105 us: state_step(): incoming = lax.ppermute(state[1], 'cp', shift)]
    reduce_sum x6 -> x0, other arithmetic: 104 us -> none  [the longest x4 65.6 us: softmax_update(): run_total = run_total * factor + jnp.sum(prob_vals, axis=-1)]
    convert_element_type x3 -> x2, other arithmetic: 41.8 us -> 2.83 us  [the longest x1 2.83 us: body(): keys = keys.astype(BF16).reshape(n_batch, n_tok, kv_width)]
    unnamed x82 -> x5, local copies, waits for them, and re-layouts: 48 us -> 17 us
  transfers between devices with their start and end apart: 11 -> 1, of which waited for: 11 -> 0; matrix products, arithmetic and copies ran while one was open for 0% -> 4% of each run, Pallas kernels for 0% -> 0%
where the time goes in v1:
time: 1210 us
  Pallas kernels  1090 us (90%)
  matrix products  68.3 us (6%)
  local copies, waits for them, and re-layouts  27.8 us (2%)
  between operations  13.5 us (1%)
    pallas_call x1, Pallas kernels, fused_layers(): pl.pallas_call(functools.partial(fused_kernel, n_tp, n_cp), out_shape=[ja...  913 us
    pallas_call x1, Pallas kernels, attention(): pl.pallas_call(functools.partial(attention_kernel, 1.0 / math.sqrt(HEAD),...  179 us
    dot_general x3, matrix products, dot(): return jnp.dot(lhs, rhs, preferred_element_type=F32)  68.3 us
  transfers between devices with their start and end apart: 1, of which 0 were waited for; matrix products, arithmetic and copies ran while one was open for 4% of the time, Pallas kernels for 0%

profile of v1, /device:TPU:5, one launch (start us, length us, event | category | flops | bytes accessed | tf_op | source)
XLA Modules:
  0.0 1208.9 jit_solution(8743851224304646461)
XLA Ops:
  6.5 0.0 all-gather.3.cloned.1.call-start
  6.5 4.6 copy.27
  11.2 9.9 fusion
  21.1 1.0 fusion.6
  22.1 1.3 fusion.7
  23.3 0.1 pad.14.clone
  23.4 0.1 pad.7.clone
  23.5 1.5 multiply_cosine_fusion
  25.0 0.1 copy.23
  25.2 1.3 maximum_maximum_fusion
  26.5 0.8 copy.22
  27.3 0.8 copy.24
  28.1 2.8 fusion.4
  30.9 1.4 copy.25
  32.3 9.9 convolution_convert_fusion
  42.2 0.0 copy-start
  42.2 0.0 copy-start.1
  42.2 1.3 pad_maximum_fusion
  43.5 0.0 all-gather.3.cloned.1.call-update
  43.5 0.0 copy-done
  43.5 0.0 copy-done.1
  43.6 0.7 broadcast_in_dim.21.gains
  44.3 48.5 %fusion.8.q_ref = f32[1536,2048]{1,0:T(8,128)} fusion(bf16[1536,6144]{1,0:T(8,128)(2,1)} %bitcast.30, bf16[6144,2048]{1,0:T(8,128)(2,1)} %param.17), kind=kOutput, calls=%fused_computation.19 | convolution fusion | flops 38654705664 | bytes 56623104 | tf_op jit(solution)/shard_map/dot_general | solution.py:28
  92.8 0.0 all-gather.3.cloned.1.call-done
  92.8 178.8 %shard_map.145.att = bf16[1536,2048]{1,0:T(8,128)(2,1)} custom-call(f32[1536,2048]{1,0:T(8,128)} %fusion.8.q_ref, bf16[4,4,384,512]{3,2,1,0:T(8,128)(2,1)} %bitcast.32, bf16[4,4,384,512]{3,2,1,0:T(8,128)(2,1)} %bitcast.33, f32[384,128]{1,0:T(8,128)S(1)} %get-tuple-element.14.same_ref, f32[384,128]{1,0:T(8,128)S(1)} %concatenate.22.right_ref, ...), custom_call_target="tpu_custom_call" | custom-call | flops 12079595520 | bytes 18874368 | tf_op jit(solution)/shard_map/pallas_call | solution.py:94
  271.7 913.4 %shard_map.146 = (bf16[1536,6144]{1,0:T(8,128)(2,1)}, bf16[1536,6144]{1,0:T(8,128)(2,1)}) custom-call(bf16[1536,2048]{1,0:T(8,128)(2,1)} %shard_map.145.att, bf16[1536,6144]{1,0:T(8,128)(2,1)} %bitcast.31, bf16[2048,6144]{1,0:T(8,128)(2,1)} %wo_a.1, bf16[6144,2048]{1,0:T(8,128)(2,1)} %wk.1, bf16[6144,2048]{1,0:T(8,128)(2,1)} %wv.1, bf16[6144,2048]{1,0:T(8,128)(2,1)} %wq.1, ...), custom_call_target="tpu_custom_call" | custom-call | flops 231928233984 | bytes 113246208 | tf_op jit(solution)/shard_map/pallas_call | solution.py:683
  1185.1 17.0 %copy.29 = bf16[4,384,6144]{2,1,0:T(8,128)(2,1)} copy(bf16[4,384,6144]{2,1,0:T(8,128)(2,1)} %bitcast.22) | data formatting | bytes 37748736
  (8 shorter events, 0.1 us)
Async XLA Ops:
  6.5 86.3 %all-gather.3.cloned.1.call-start = ((), (), s32[]{:S(2)}) async-start(), calls=%async_computation | async-start | bytes 7864320 | tf_op jit(solution)/shard_map/all_gather | solution.py:710
  42.2 1.3 copy-start
  42.2 1.3 copy-start.1
Sparse Core Ops, SparseCore 0:
  43.7 46.8 all-gather.2

commit v2 on v1

--- a/solution.py
+++ b/solution.py
@@ -3,6 +3,7 @@
 
 import jax
 import jax.numpy as jnp
+import numpy as np
 from jax import lax
 from jax.experimental import pallas as pl
 from jax.experimental.pallas import tpu as pltpu
@@ -32,101 +33,45 @@
     return lax.dot_general(lhs, rhs, (((1,), (1,)), ((), ())), preferred_element_type=F32)
 
 
-def rotary_tables(positions):
-    rot = HEAD // 2
-    half = rot // 2
-    inv_freq = jnp.power(ROPE_BASE, -jnp.arange(half, dtype=F32) * 2.0 / rot)
-    angles = positions.astype(F32)[:, None] * inv_freq[None, :]
-    cosine, sine = jnp.cos(angles), jnp.sin(angles)
-    n = positions.shape[0]
-    same = jnp.concatenate([cosine, cosine, jnp.ones((n, HEAD - rot), F32)], axis=1)
-    from_right = jnp.concatenate([-sine, jnp.zeros((n, HEAD - half), F32)], axis=1)
-    from_left = jnp.concatenate([jnp.zeros((n, half), F32), sine, jnp.zeros((n, HEAD - rot), F32)], axis=1)
-    return same, from_right, from_left
-
-
-def attention_kernel(scale, n_heads, q_ref, k_ref, v_ref, same_ref, right_ref, left_ref, o_ref, acc, top, total):
-    blk = lax.axis_index("cp")
-    n_tok = q_ref.shape[0]
-    quarter = HEAD // 4
-
-    def head(h, carry):
-        cols = pl.ds(pl.multiple_of(h * HEAD, HEAD), HEAD)
-        raw = q_ref[:, cols]
-        turned = raw * same_ref[...] + pltpu.roll(raw, HEAD - quarter, 1) * right_ref[...]
-        query = (turned + pltpu.roll(raw, quarter, 1) * left_ref[...]).astype(BF16)
-
-        scores = dot_t(query, k_ref[blk]) * scale
-        rows = lax.broadcasted_iota(jnp.int32, scores.shape, 0)
-        keys = lax.broadcasted_iota(jnp.int32, scores.shape, 1)
-        scores = jnp.where(rows >= keys, scores, -jnp.inf)
-        peak = jnp.max(scores, axis=-1, keepdims=True)
-        probs = jnp.exp(scores - peak)
-        top[...] = jnp.broadcast_to(peak, (n_tok, HEAD))
-        total[...] = jnp.broadcast_to(jnp.sum(probs, axis=-1, keepdims=True), (n_tok, HEAD))
-        acc[...] = dot(probs.astype(BF16), v_ref[blk])
-
-        def earlier(j, inner):
-            later_scores = dot_t(query, k_ref[j]) * scale
-            old = top[:, 0:1]
-            new = jnp.maximum(old, jnp.max(later_scores, axis=-1, keepdims=True))
-            factor = jnp.exp(old - new)
-            vals = jnp.exp(later_scores - new)
-            top[...] = jnp.broadcast_to(new, (n_tok, HEAD))
-            total[...] = total[...] * factor + jnp.sum(vals, axis=-1, keepdims=True)
-            acc[...] = acc[...] * factor + dot(vals.astype(BF16), v_ref[j])
-            return inner
-
-        lax.fori_loop(0, blk, earlier, 0)
-        o_ref[:, cols] = (acc[...] / total[...]).astype(BF16)
-        return carry
-
-    lax.fori_loop(0, n_heads, head, 0)
-
-
-def attention(q_proj, kv_all, tables, n_tok):
-    n_rows, width = q_proj.shape
-    n_batch = n_rows // n_tok
-    n_cp = kv_all.shape[0]
-    kv_heads = kv_all.shape[3] // (2 * HEAD)
-    per_kv = width // kv_heads
-    table = pl.BlockSpec((n_tok, HEAD), lambda b, g: (0, 0))
-    return pl.pallas_call(
-        functools.partial(attention_kernel, 1.0 / math.sqrt(HEAD), per_kv // HEAD),
-        out_shape=jax.ShapeDtypeStruct((n_rows, width), BF16),
-        grid=(n_batch, kv_heads),
-        in_specs=[
-            pl.BlockSpec((n_tok, per_kv), lambda b, g: (b, g)),
-            pl.BlockSpec((n_cp, None, n_tok, HEAD), lambda b, g: (0, b, 0, g)),
-            pl.BlockSpec((n_cp, None, n_tok, HEAD), lambda b, g: (0, b, 0, kv_heads + g)),
-            table,
-            table,
-            table,
-        ],
-        out_specs=pl.BlockSpec((n_tok, per_kv), lambda b, g: (b, g)),
-        scratch_shapes=[pltpu.VMEM((n_tok, HEAD), F32)] * 3,
-        compiler_params=pltpu.CompilerParams(vmem_limit_bytes=48 * 1024 * 1024),
-        cost_estimate=pl.CostEstimate(flops=2 * n_rows * width * n_tok * 5, bytes_accessed=n_rows * width * 6, transcendentals=0),
-    )(q_proj, kv_all, kv_all, *tables)
+def rotary_table(n_pos):
+    half = HEAD // 4
+    inv_freq = np.power(ROPE_BASE, -np.arange(half) * 2.0 / (2 * half)).astype(np.float32)
+    angles = (np.arange(n_pos, dtype=np.float32)[:, None] * inv_freq[None, :]).astype(np.float64)
+    cosine, sine = np.cos(angles), np.sin(angles)
+    return np.concatenate([cosine, cosine, sine, sine], axis=1).astype(np.float32)
+
+
+def fold(vals, op, reduce, share):
+    n_cols = vals.shape[1]
+    if n_cols % HEAD:
+        return jnp.broadcast_to(reduce(vals, axis=-1, keepdims=True) * share, (vals.shape[0], HEAD))
+    out = vals[:, 0:HEAD]
+    for k in range(1, n_cols // HEAD):
+        out = op(out, vals[:, k * HEAD : (k + 1) * HEAD])
+    return out
 
 
 def fused_kernel(
     n_tp,
     n_cp,
-    att,
     hid,
+    wk_a,
+    wv_a,
+    wq_a,
     wo_a,
     wk,
     wv,
     wq,
     wg,
     wo_l,
+    table,
     gains,
     ginner,
     alphas,
     slopes,
     out,
     h1,
+    kv_all,
     part,
     summed,
     normed,
@@ -145,6 +90,10 @@
     row_inv,
     sq_send,
     sq_recv,
+    kv_own,
+    kv_buf,
+    rope,
+    sums,
     reduce_send,
     reduce_recv,
     back_send,
@@ -153,7 +102,11 @@
     out_sem,
     w_sem,
     wo_sem,
-    y_sem,
+    hid_sem,
+    rope_sem,
+    kv_send,
+    kv_recv,
+    kv_load,
     state_send,
     state_recv,
     sq_send_sem,
@@ -163,7 +116,10 @@
     _, n_tok, model = part.shape
     width = y_buf.shape[1]
     n_heads = width // HEAD
-    n_batch = att.shape[0] // n_tok
+    n_batch = hid.shape[0] // n_tok
+    kv_width = wk_a.shape[1]
+    group = width // kv_width
+    n_pairs = n_heads // 2
     half = n_tok // 2
     rows = res.shape[2]
     per_batch = half // rows
@@ -173,32 +129,79 @@
     w_cols = w_buf.shape[2]
     wo_cols = wo_buf.shape[2]
     n_wo = model // wo_cols
+    kv_tiles = kv_width // w_cols
+    a_tiles = 2 * kv_tiles + 8
     last = n_tp - 1
     trip = 2 * last * LEAD
     z = lax.axis_index("tp")
     c = lax.axis_index("cp")
 
+    def hidden_copy(batch):
+        at = lax.rem(batch, 2)
+        return pltpu.make_async_copy(hid.at[pl.ds(pl.multiple_of(batch * n_tok, n_tok), n_tok), :], normed.at[at], hid_sem.at[at])
+
+    def a_tile(unit):
+        phase = lax.div(unit, UNITS) - 1
+        r = lax.rem(unit, UNITS)
+        late = r >= 12
+        j = jnp.where(late, r - 12, r)
+        is_a = (phase <= 1) & (j < a_tiles) & (jnp.logical_not(late) | (phase == 0))
+        batch = jnp.where(phase == 1, 3, jnp.where(late, 2, phase + 1))
+        return is_a, batch, j
+
+    def w_cut(weight, tile, slot):
+        cols = pl.ds(pl.multiple_of(tile * w_cols, w_cols), w_cols)
+        return pltpu.make_async_copy(weight.at[:, cols], w_buf.at[slot], w_sem.at[slot])
+
+    def fetch(unit):
+        slot = lax.rem(unit, W_SLOTS)
+        r = lax.rem(unit, UNITS)
+        is_a, _, j = a_tile(unit)
+
+        @pl.when(is_a & (j < kv_tiles))
+        def _():
+            w_cut(wk_a, j, slot).start()
+
+        @pl.when(is_a & (j >= kv_tiles) & (j < 2 * kv_tiles))
+        def _():
+            w_cut(wv_a, j - kv_tiles, slot).start()
+
+        @pl.when(is_a & (j >= 2 * kv_tiles))
+        def _():
+            w_cut(wq_a, j - 2 * kv_tiles, slot).start()
+
+        @pl.when(has_projection(lax.div(unit, UNITS) - 1))
+        def _():
+            for k, weight in enumerate((wk, wv, wq, wg)):
+
+                @pl.when(lax.div(r, 8) == k)
+                def _():
+                    w_cut(weight, lax.rem(r, 8), slot).start()
+
+    def has_projection(phase):
+        return (phase >= 2) & (phase < 2 + n_batch)
+
+    for i in range(2):
+        hidden_copy(i).start()
+    for i in range(W_SLOTS):
+        fetch(jnp.int32(i))
+    table_copy = pltpu.make_async_copy(table.at[pl.ds(pl.multiple_of(c * n_tok, n_tok), n_tok), :], rope.at[0], rope_sem)
+    table_copy.start()
+
     barrier = pltpu.get_barrier_semaphore()
     for k in range(1, n_tp):
         pl.semaphore_signal(barrier, inc=1, device_id={"tp": lax.rem(z + k, n_tp)}, device_id_type=MESH)
-
-    @pl.when(c > 0)
-    def _():
-        pl.semaphore_signal(barrier, inc=1, device_id={"cp": c - 1}, device_id_type=MESH)
-
-    @pl.when(c < n_cp - 1)
-    def _():
-        pl.semaphore_signal(barrier, inc=1, device_id={"cp": c + 1}, device_id_type=MESH)
-
-    inner = (c > 0) & (c < n_cp - 1)
-
-    @pl.when(inner)
-    def _():
-        pl.semaphore_wait(barrier, n_tp + 1)
-
-    @pl.when(jnp.logical_not(inner))
-    def _():
-        pl.semaphore_wait(barrier, n_tp)
+    for k in range(1, n_cp):
+        pl.semaphore_signal(barrier, inc=1, device_id={"cp": lax.rem(c + k, n_cp)}, device_id_type=MESH)
+
+    table_copy.wait()
+    lane = lax.broadcasted_iota(jnp.int32, (n_tok, HEAD), 1)
+    cosines = rope[0]
+    sines = pltpu.roll(cosines, HEAD // 2, 1)
+    rope[0] = jnp.where(lane < HEAD // 2, cosines, 1.0)
+    rope[1] = jnp.where(lane < HEAD // 4, -sines, 0.0)
+    rope[2] = jnp.where((lane >= HEAD // 4) & (lane < HEAD // 2), sines, 0.0)
+    pl.semaphore_wait(barrier, n_tp + n_cp - 2)
 
     def row_of(g, f):
         return pl.multiple_of(f * half + lax.rem(g, per_batch) * rows, rows)
@@ -366,35 +369,27 @@
                 def _():
                     out_copy(done, f, out).start()
 
-    projections = (wk, wv, wq, wg)
-
-    def w_copy(which, tile, slot):
-        cols = pl.ds(pl.multiple_of(tile * w_cols, w_cols), w_cols)
-        return pltpu.make_async_copy(projections[which].at[:, cols], w_buf.at[slot], w_sem.at[slot])
-
     def wo_copy(weight, tile):
         cols = pl.ds(pl.multiple_of(tile * wo_cols, wo_cols), wo_cols)
         slot = lax.rem(tile, 2)
         return pltpu.make_async_copy(weight.at[:, cols], wo_buf.at[slot], wo_sem.at[slot])
 
-    def has_projection(phase):
-        return (phase >= 2) & (phase < 2 + n_batch)
-
-    def project(unit, phase, which, tile):
+    def project(unit, at):
         slot = lax.rem(unit, W_SLOTS)
-        w_copy(0, tile, slot).wait()
-        at = lax.rem(phase, 2)
+        w_cut(wk, 0, slot).wait()
         depth = model // 6
-        acc[:, 0:w_cols] = jnp.zeros((n_tok, w_cols), F32)
+        acc[...] = jnp.zeros_like(acc)
 
         def chunk(i, carry):
             ks = pl.ds(pl.multiple_of(i * depth, depth), depth)
-            acc[:, 0:w_cols] += dot(normed[at, :, ks], w_buf[slot, ks, :])
+            acc[...] += dot(normed[at, :, ks], w_buf[slot, ks, :])
             return carry
 
         lax.fori_loop(0, 6, chunk, 0)
+
+    def store_b(which, tile):
         cols = pl.ds(pl.multiple_of(tile * w_cols, w_cols), w_cols)
-        vals = acc[:, 0:w_cols]
+        vals = acc[...]
         soft = jax.nn.sigmoid(vals)
 
         @pl.when(which < 3)
@@ -404,6 +399,136 @@
         @pl.when(which == 3)
         def _():
             gate[:, cols] = soft
+
+    def query_slot(batch):
+        return jnp.where(batch == 3, 2, lax.rem(batch, 2))
+
+    def store_a(batch, j):
+        @pl.when((j >= kv_tiles) & (j < 2 * kv_tiles))
+        def _():
+            cols = pl.ds(pl.multiple_of(j * w_cols, w_cols), w_cols)
+            kv_own[:, cols] = acc[...].astype(BF16)
+
+        @pl.when((j < kv_tiles) | (j >= 2 * kv_tiles))
+        def _():
+            for e in range(w_cols // HEAD):
+                raw = acc[:, e * HEAD : (e + 1) * HEAD]
+                turned = raw * rope[0] + pltpu.roll(raw, HEAD - HEAD // 4, 1) * rope[1]
+                turned = (turned + pltpu.roll(raw, HEAD // 4, 1) * rope[2]).astype(BF16)
+
+                @pl.when(j < kv_tiles)
+                def _():
+                    kv_own[:, pl.ds(pl.multiple_of(j * w_cols + e * HEAD, HEAD), HEAD)] = turned
+
+                @pl.when(j >= 2 * kv_tiles)
+                def _():
+                    cols = pl.ds(pl.multiple_of((j - 2 * kv_tiles) * w_cols + e * HEAD, HEAD), HEAD)
+                    kvq[query_slot(batch), :, cols] = turned
+
+        @pl.when(j == 2 * kv_tiles - 1)
+        def _():
+            kv_store(batch).start()
+            for k in range(1, n_cp):
+
+                @pl.when(c + k < n_cp)
+                def _():
+                    kv_copy(batch, k).start()
+
+    def kv_store(batch):
+        return pltpu.make_async_copy(kv_own, kv_all.at[batch, c], kv_load.at[n_cp])
+
+    def kv_copy(batch, k):
+        return pltpu.make_async_remote_copy(
+            src_ref=kv_own,
+            dst_ref=kv_all.at[batch, c],
+            send_sem=kv_send.at[k],
+            recv_sem=kv_recv.at[batch, c],
+            device_id={"cp": c + k},
+            device_id_type=MESH,
+        )
+
+    def kv_arrival(batch, source):
+        return pltpu.make_async_remote_copy(
+            src_ref=kv_own,
+            dst_ref=kv_all.at[batch, source],
+            send_sem=kv_send.at[0],
+            recv_sem=kv_recv.at[batch, source],
+            device_id={"cp": source},
+            device_id_type=MESH,
+        )
+
+    def kv_fetch(batch, source):
+        return pltpu.make_async_copy(kv_all.at[batch, source], kv_buf.at[source], kv_load.at[source])
+
+    def load_kv(batch):
+        kv_store(batch).wait()
+        for k in range(1, n_cp):
+
+            @pl.when(c + k < n_cp)
+            def _():
+                kv_copy(batch, k).wait_send()
+
+        for source in range(n_cp):
+
+            @pl.when(source < c)
+            def _():
+                kv_arrival(batch, source).wait_recv()
+
+            @pl.when(source <= c)
+            def _():
+                kv_fetch(batch, source).start()
+
+        for source in range(n_cp):
+
+            @pl.when(source <= c)
+            def _():
+                kv_fetch(batch, source).wait()
+
+    def attend(batch, pair):
+        kv_head = lax.div(2 * pair, group)
+        key_cols = pl.ds(pl.multiple_of(kv_head * HEAD, HEAD), HEAD)
+        value_cols = pl.ds(pl.multiple_of(kv_width + kv_head * HEAD, HEAD), HEAD)
+        head_cols = [pl.ds(pl.multiple_of((2 * pair + e) * HEAD, HEAD), HEAD) for e in range(2)]
+        at = query_slot(batch)
+        score_refs = (o_buf, gate)
+        top_refs = (sq_acc, row_inv)
+        power = math.log2(math.e) / math.sqrt(HEAD)
+
+        def span(j):
+            return pl.ds(pl.multiple_of(j * n_tok, n_tok), n_tok)
+
+        rows_at = lax.broadcasted_iota(jnp.int32, (n_tok, n_tok), 0)
+        keys_at = lax.broadcasted_iota(jnp.int32, (n_tok, n_tok), 1)
+        for e in range(2):
+            scores = dot_t(kvq[at, :, head_cols[e]], kv_buf[c, :, key_cols])
+            scores = jnp.where(rows_at >= keys_at, scores, -jnp.inf)
+            score_refs[e][:, span(c)] = scores
+            top_refs[e][...] = fold(scores, jnp.maximum, jnp.max, 1.0)
+
+        def score(j, carry):
+            for e in range(2):
+                scores = dot_t(kvq[at, :, head_cols[e]], kv_buf[j, :, key_cols])
+                score_refs[e][:, span(j)] = scores
+                top_refs[e][...] = jnp.maximum(top_refs[e][...], fold(scores, jnp.maximum, jnp.max, 1.0))
+            return carry
+
+        lax.fori_loop(0, c, score, 0)
+        for e in range(2):
+            top_refs[e][...] = jnp.broadcast_to(jnp.max(top_refs[e][...], axis=-1, keepdims=True), (n_tok, HEAD))
+            sums[e] = jnp.zeros((n_tok, HEAD), F32)
+            acc[:, e * HEAD : (e + 1) * HEAD] = jnp.zeros((n_tok, HEAD), F32)
+
+        def weigh(j, carry):
+            for e in range(2):
+                probs = jnp.exp2((score_refs[e][:, span(j)] - top_refs[e][:, 0:1]) * power)
+                sums[e] += fold(probs, jnp.add, jnp.sum, 1.0 / HEAD)
+                acc[:, e * HEAD : (e + 1) * HEAD] += dot(probs.astype(BF16), kv_buf[j, :, value_cols])
+            return carry
+
+        lax.fori_loop(0, c + 1, weigh, 0)
+        for e in range(2):
+            total = jnp.sum(sums[e], axis=-1, keepdims=True)
+            y_buf[:, head_cols[e]] = (acc[:, e * HEAD : (e + 1) * HEAD] / total).astype(BF16)
 
     def out_project(phase, tile):
         wo_copy(wo_a, tile).wait()
@@ -550,10 +675,34 @@
             else:
                 lax.fori_loop(0, per_group // 3, one, 0)
 
-        @pl.when((r == 8) & first_layer)
-        def _():
-            batch_rows = pl.ds(pl.multiple_of((phase + 1) * n_tok, n_tok), n_tok)
-            pltpu.make_async_copy(att.at[batch_rows, :], y_buf, y_sem).start()
+        for at_phase, at_r, batch in ((0, 0, 1), (0, 12, 2), (1, 0, 3)):
+
+            @pl.when((phase == at_phase) & (r == at_r))
+            def _():
+                hidden_copy(batch).wait()
+
+        for at_phase, batch in ((-1, 2), (0, 3)):
+
+            @pl.when((phase == at_phase) & (r == 12))
+            def _():
+                hidden_copy(batch).start()
+
+        @pl.when(first_layer & (r == jnp.where(phase <= 0, 12, 0)))
+        def _():
+            load_kv(phase + 1)
+
+        early = phase <= 0
+        spread = 16 // n_pairs
+        first_pair = jnp.where(early, (r - 12) * (n_pairs // 4), lax.div(r, spread))
+        n_here = jnp.where(early, jnp.where(r >= 12, n_pairs // 4, 0), jnp.where(lax.rem(r, spread) == 0, 1, 0))
+
+        @pl.when(first_layer & (r < 16))
+        def _():
+            def one_pair(i, inner):
+                attend(phase + 1, first_pair + i)
+                return inner
+
+            lax.fori_loop(0, n_here, one_pair, 0)
 
         for i in range(2):
 
@@ -579,10 +728,6 @@
         def _():
             finish_lightning(phase - 3)
 
-        @pl.when((r == 16) & first_layer)
-        def _():
-            pltpu.make_async_copy(att.at[pl.ds(0, n_tok), :], y_buf, y_sem).wait()
-
         wo_tile = r - 16
 
         @pl.when((wo_tile >= 0) & (wo_tile < n_wo) & (first_layer | second_layer))
@@ -597,20 +742,21 @@
             def _():
                 wo_copy(wo_l, wo_tile + 2).start()
 
-        @pl.when(projects)
-        def _():
-            project(unit, phase, which, tile)
-
-        coming = unit + W_SLOTS
-        coming_r = lax.rem(coming, UNITS)
-
-        @pl.when(has_projection(lax.div(coming, UNITS) - 1))
-        def _():
-            for k in range(4):
-
-                @pl.when(lax.div(coming_r, 8) == k)
-                def _():
-                    w_copy(k, lax.rem(coming_r, 8), lax.rem(coming, W_SLOTS)).start()
+        is_a, a_batch, a_j = a_tile(unit)
+
+        @pl.when(is_a | projects)
+        def _():
+            project(unit, jnp.where(is_a, lax.rem(a_batch, 2), lax.rem(phase, 2)))
+
+            @pl.when(is_a)
+            def _():
+                store_a(a_batch, a_j)
+
+            @pl.when(projects)
+            def _():
+                store_b(which, tile)
+
+        fetch(unit + W_SLOTS)
 
         @pl.when((r == 23) & projects)
         def _():
@@ -628,6 +774,7 @@
 
         return carry
 
+    hidden_copy(0).wait()
     n_phases = 2 * n_batch + 2
     lax.fori_loop(0, n_phases * UNITS, unit_body, 0)
     for f in range(2):
@@ -635,10 +782,20 @@
             out_copy(pieces - 4 + k, f, out).wait()
 
 
-def fused_layers(att, hid, weights, gains, ginner, alphas, slopes, n_tok, n_tp, n_cp):
-    wo_a, wk, wv, wq, wg, wo_l = weights
-    n_rows, width = att.shape
-    model = hid.shape[1]
+def copy_kernel(src, dst):
+    dst[...] = src[...]
+
+
+def plain_copy(array, blocks):
+    n_rows, n_cols = array.shape
+    spec = pl.BlockSpec((n_rows // blocks, n_cols), lambda i: (i, 0))
+    return pl.pallas_call(copy_kernel, out_shape=jax.ShapeDtypeStruct(array.shape, array.dtype), grid=(blocks,), in_specs=[spec], out_specs=spec)(array)
+
+
+def fused_layers(hid, weights, gains, ginner, alphas, slopes, n_tok, n_tp, n_cp):
+    n_rows, model = hid.shape
+    width = weights[2].shape[1]
+    kv_width = weights[0].shape[1]
     n_batch = n_rows // n_tok
     n_heads = width // HEAD
     rows = n_tok // 24
@@ -659,11 +816,15 @@
         vmem((n_heads, HEAD, HEAD), F32),
         vmem((2, 4, rows, model), BF16),
         vmem((rows, model), F32),
-        vmem((n_tok, max(w_cols, HEAD)), F32),
+        vmem((n_tok, w_cols), F32),
         vmem((n_tok, HEAD), F32),
         vmem((n_tok, HEAD), F32),
         vmem((8, n_tok), F32),
         vmem((n_batch, n_tp, 8, n_tok), F32),
+        vmem((n_tok, 2 * kv_width), BF16),
+        vmem((n_cp, n_tok, 2 * kv_width), BF16),
+        vmem((3, n_tok, HEAD), F32),
+        vmem((2, n_tok, HEAD), F32),
         dma((2, RING)),
         dma((2, RING)),
         dma((2, RING)),
@@ -672,23 +833,31 @@
         dma((2, 4)),
         dma((W_SLOTS,)),
         dma((2,)),
+        dma((2,)),
         dma,
+        dma((n_cp,)),
+        dma((n_batch, n_cp)),
+        dma((n_cp + 1,)),
         dma,
         dma,
         dma((n_tp,)),
         dma((n_batch, n_tp)),
         pltpu.SemaphoreType.REGULAR,
     ]
-    flops = 2 * n_rows * model * width * 6
+    flops = 2 * n_rows * model * width * 8
     return pl.pallas_call(
         functools.partial(fused_kernel, n_tp, n_cp),
-        out_shape=[jax.ShapeDtypeStruct((n_rows, model), BF16)] * 2,
-        in_specs=[ANY] * 8 + [VMEM] * 2 + [SMEM] * 2,
-        out_specs=[ANY] * 2,
+        out_shape=[
+            jax.ShapeDtypeStruct((n_rows, model), BF16),
+            jax.ShapeDtypeStruct((n_rows, model), BF16),
+            jax.ShapeDtypeStruct((n_batch, n_cp, n_tok, 2 * kv_width), BF16),
+        ],
+        in_specs=[ANY] * 11 + [VMEM] * 2 + [SMEM] * 2,
+        out_specs=[ANY] * 3,
         scratch_shapes=scratch,
         compiler_params=pltpu.CompilerParams(collective_id=0, has_side_effects=True, vmem_limit_bytes=67043328),
         cost_estimate=pl.CostEstimate(flops=flops, bytes_accessed=12 * n_rows * model, transcendentals=0),
-    )(att, hid, wo_a, wk, wv, wq, wg, wo_l, gains, ginner, alphas, slopes)
+    )(hid, *weights, rotary_table(n_tok * n_cp), gains, ginner, alphas, slopes)
 
 
 def solution(mesh):
@@ -697,24 +866,10 @@
     def body(hidden, alphas, wq_attn, wk_attn, wv_attn, wo_attn, gain_attn, wq_lin, wk_lin, wv_lin, wg_lin, slopes, gain_inner, wo_lin, gain_lin):
         n_batch, n_tok, model = hidden.shape
         flat = hidden.reshape(n_batch * n_tok, model)
-        kv_width = wk_attn.shape[1]
-        positions = lax.axis_index("cp") * n_tok + jnp.arange(n_tok)
-        tables = rotary_tables(positions)
-
-        k_proj = dot(flat, wk_attn).reshape(n_batch, n_tok, kv_width // HEAD, HEAD)
-        same, from_right, from_left = (t[None, :, None, :] for t in tables)
-        quarter = HEAD // 4
-        keys = k_proj * same + jnp.roll(k_proj, -quarter, axis=-1) * from_right + jnp.roll(k_proj, quarter, axis=-1) * from_left
-        keys = keys.astype(BF16).reshape(n_batch, n_tok, kv_width)
-        values = dot(flat, wv_attn).astype(BF16).reshape(n_batch, n_tok, kv_width)
-        kv_all = lax.all_gather(jnp.concatenate([keys, values], axis=-1), "cp")
-
-        q_proj = dot(flat, wq_attn)
-        att = attention(q_proj, kv_all, tables, n_tok)
         gains = jnp.stack([gain_attn, gain_lin])[:, None, :]
-        weights = (wo_attn, wk_lin, wv_lin, wq_lin, wg_lin, wo_lin)
-        out, _ = fused_layers(att, flat, weights, gains, gain_inner.reshape(-1, 1, HEAD), alphas, slopes, n_tok, n_tp, n_cp)
-        return out.reshape(hidden.shape)
+        weights = (wk_attn, wv_attn, wq_attn, wo_attn, wk_lin, wv_lin, wq_lin, wg_lin, wo_lin)
+        outs = fused_layers(flat, weights, gains, gain_inner.reshape(-1, 1, HEAD), alphas, slopes, n_tok, n_tp, n_cp)
+        return plain_copy(outs[0], 12).reshape(hidden.shape)
 
     act_spec = P("dp", "cp", None)
     rep_spec = P()

time: 1210 us -> 1080 us (0.89)
  matrix products: 68.3 us -> 0 us
  local copies, waits for them, and re-layouts: 27.8 us -> 0.65 us
  between operations: 13.5 us -> 0.01 us
    pallas_call x1, Pallas kernels: 179 us -> 16.8 us  [plain_copy(): pl.pallas_call(copy_kernel, out_shape=jax.ShapeDtypeStruct(array.shape, a...]
    pallas_call x1, Pallas kernels: 913 us -> 1060 us  [fused_layers(): pl.pallas_call(functools.partial(fused_kernel, n_tp, n_cp), out_shape=[ja...]
    dot_general x3 -> x0, matrix products: 68.3 us -> none  [dot(): return jnp.dot(lhs, rhs, preferred_element_type=F32)]
    unnamed x5 -> x0, local copies, waits for them, and re-layouts: 17 us -> none
  transfers between devices with their start and end apart: 1 -> 0, of which waited for: 0 -> 0; matrix products, arithmetic and copies ran while one was open for 4% -> 0% of each run, Pallas kernels for 0% -> 0%
where the time goes in v2:
time: 1080 us
  Pallas kernels  1080 us (100%)
    pallas_call x1, Pallas kernels, fused_layers(): pl.pallas_call(functools.partial(fused_kernel, n_tp, n_cp), out_shape=[ja...  1060 us

profile of v2, /device:TPU:5, one launch (start us, length us, event | category | flops | bytes accessed | tf_op | source)
XLA Modules:
  0.0 1077.6 jit_solution(1685253973342565685)
XLA Ops:
  0.0 0.8 pad_maximum_fusion
  0.8 0.7 broadcast_in_dim.3.gains
  1.5 1059.3 %shard_map.154 = (bf16[1536,6144]{1,0:T(8,128)(2,1)}, bf16[1536,6144]{1,0:T(8,128)(2,1)}, bf16[4,4,384,512]{3,2,1,0:T(8,128)(2,1)}) custom-call(bf16[1536,6144]{1,0:T(8,128)(2,1)} %bitcast.7, bf16[6144,256]{1,0:T(8,128)(2,1)} %wk_a.1, bf16[6144,256]{1,0:T(8,128)(2,1)} %wv_a.1, bf16[6144,2048]{1,0:T(8,128)(2,1)} %wq_a.1, bf16[2048,6144]{1,0:T(8,128)(2,1)} %wo_a.1, ...), custom_call_target="tpu_custom_call" | custom-call | flops 309237645312 | bytes 113246208 | tf_op jit(solution)/shard_map/pallas_call | solution.py:848
  1060.8 16.8 %shard_map.155 = bf16[1536,6144]{1,0:T(8,128)(2,1)} custom-call(bf16[1536,6144]{1,0:T(8,128)(2,1)} %get-tuple-element.6.src), custom_call_target="tpu_custom_call" | custom-call | tf_op jit(solution)/shard_map/pallas_call | solution.py:792

commit v3 on v2

--- a/solution.py
+++ b/solution.py
@@ -65,7 +65,8 @@
     wg,
     wo_l,
     table,
-    gains,
+    gain_a,
+    gain_l,
     ginner,
     alphas,
     slopes,
@@ -85,6 +86,7 @@
     state_in,
     res,
     wide,
+    gains,
     acc,
     sq_acc,
     row_inv,
@@ -119,7 +121,6 @@
     n_batch = hid.shape[0] // n_tok
     kv_width = wk_a.shape[1]
     group = width // kv_width
-    n_pairs = n_heads // 2
     half = n_tok // 2
     rows = res.shape[2]
     per_batch = half // rows
@@ -143,8 +144,8 @@
     def a_tile(unit):
         phase = lax.div(unit, UNITS) - 1
         r = lax.rem(unit, UNITS)
-        late = r >= 12
-        j = jnp.where(late, r - 12, r)
+        late = r >= 20
+        j = jnp.where(late, r - 20, r)
         is_a = (phase <= 1) & (j < a_tiles) & (jnp.logical_not(late) | (phase == 0))
         batch = jnp.where(phase == 1, 3, jnp.where(late, 2, phase + 1))
         return is_a, batch, j
@@ -156,21 +157,27 @@
     def fetch(unit):
         slot = lax.rem(unit, W_SLOTS)
         r = lax.rem(unit, UNITS)
-        is_a, _, j = a_tile(unit)
-
-        @pl.when(is_a & (j < kv_tiles))
-        def _():
-            w_cut(wk_a, j, slot).start()
-
-        @pl.when(is_a & (j >= kv_tiles) & (j < 2 * kv_tiles))
-        def _():
-            w_cut(wv_a, j - kv_tiles, slot).start()
-
-        @pl.when(is_a & (j >= 2 * kv_tiles))
-        def _():
-            w_cut(wq_a, j - 2 * kv_tiles, slot).start()
-
-        @pl.when(has_projection(lax.div(unit, UNITS) - 1))
+        phase = lax.div(unit, UNITS) - 1
+
+        @pl.when(phase <= 1)
+        def _():
+            is_a, _, j = a_tile(unit)
+
+            @pl.when(is_a & (j >= 2 * kv_tiles))
+            def _():
+                w_cut(wq_a, j - 2 * kv_tiles, slot).start()
+
+            @pl.when(is_a & (j < 2 * kv_tiles))
+            def _():
+                @pl.when(j < kv_tiles)
+                def _():
+                    w_cut(wk_a, j, slot).start()
+
+                @pl.when(j >= kv_tiles)
+                def _():
+                    w_cut(wv_a, j - kv_tiles, slot).start()
+
+        @pl.when(has_projection(phase))
         def _():
             for k, weight in enumerate((wk, wv, wq, wg)):
 
@@ -194,6 +201,8 @@
     for k in range(1, n_cp):
         pl.semaphore_signal(barrier, inc=1, device_id={"cp": lax.rem(c + k, n_cp)}, device_id_type=MESH)
 
+    gains[0] = gain_a[...]
+    gains[1] = gain_l[...]
     table_copy.wait()
     lane = lax.broadcasted_iota(jnp.int32, (n_tok, HEAD), 1)
     cosines = rope[0]
@@ -245,29 +254,22 @@
     def out_copy(g, f, ref):
         return pltpu.make_async_copy(view(normed, g, f), hbm_rows(ref, g, f), out_sem.at[f, lax.rem(g, 4)])
 
-    def norm_rows(g, f):
+    def norm_rows(g):
         layer = (g >= layer_pieces).astype(jnp.int32)
         slot = lax.rem(g, 4)
         at = lax.rem(lax.div(g, per_batch), 2)
-        span = pl.ds(row_of(g, f), rows)
         alpha = alphas[layer]
-        n_chunk = model // wo_cols
-
-        def first(i, sq):
-            cols = pl.ds(pl.multiple_of(i * wo_cols, wo_cols), wo_cols)
-            vals = alpha * res[f, slot, :, cols].astype(F32) + summed[at, span, cols].astype(F32)
-            wide[:, cols] = vals
-            return sq + vals * vals
-
-        sq = lax.fori_loop(0, n_chunk, first, jnp.zeros((rows, wo_cols), F32))
-        scale = lax.rsqrt(jnp.sum(sq, axis=-1, keepdims=True) / model + NORM_EPS)
-
-        def second(i, carry):
-            cols = pl.ds(pl.multiple_of(i * wo_cols, wo_cols), wo_cols)
-            normed[at, span, cols] = (wide[:, cols] * scale * gains[layer, :, cols]).astype(BF16)
-            return carry
-
-        lax.fori_loop(0, n_chunk, second, 0)
+        chunks = [slice(i * wo_cols, (i + 1) * wo_cols) for i in range(n_wo)]
+        for f in range(2):
+            span = pl.ds(row_of(g, f), rows)
+            sq = jnp.zeros((rows, wo_cols), F32)
+            for cols in chunks:
+                vals = alpha * res[f, slot, :, cols].astype(F32) + summed[at, span, cols].astype(F32)
+                wide[f, :, cols] = vals
+                sq = sq + vals * vals
+            scale = lax.rsqrt(jnp.sum(sq, axis=-1, keepdims=True) / model + NORM_EPS)
+            for cols in chunks:
+                normed[at, span, cols] = (wide[f, :, cols] * scale * gains[layer, :, cols]).astype(BF16)
 
     def known(g):
         return (g >= 0) & (g < pieces)
@@ -347,26 +349,22 @@
                 def _():
                     backward(done, f).wait_send()
 
-                @pl.when(done < layer_pieces)
-                def _():
-                    res_copy(done, f, hid).wait()
-
-                @pl.when(done >= layer_pieces)
-                def _():
-                    res_copy(done, f, h1).wait()
+                res_copy(done, f, hid).wait()
 
                 @pl.when(done >= 4)
                 def _():
                     out_copy(done - 4, f, out).wait()
 
-                norm_rows(done, f)
-
-                @pl.when(done < layer_pieces)
-                def _():
+            norm_rows(done)
+
+            @pl.when(done < layer_pieces)
+            def _():
+                for f in range(2):
                     out_copy(done, f, h1).start()
 
-                @pl.when(done >= layer_pieces)
-                def _():
+            @pl.when(done >= layer_pieces)
+            def _():
+                for f in range(2):
                     out_copy(done, f, out).start()
 
     def wo_copy(weight, tile):
@@ -374,31 +372,31 @@
         slot = lax.rem(tile, 2)
         return pltpu.make_async_copy(weight.at[:, cols], wo_buf.at[slot], wo_sem.at[slot])
 
-    def project(unit, at):
+    halves = (slice(0, half), slice(half, n_tok))
+
+    def project_a(unit, batch, j):
+        slot = lax.rem(unit, W_SLOTS)
+        at = lax.rem(batch, 2)
+        w_cut(wk, 0, slot).wait()
+        for span in halves:
+            acc[span, :] = dot(normed[at, span, :], w_buf[slot])
+        store_a(batch, j)
+
+    def project_b(unit, at, which, tile):
         slot = lax.rem(unit, W_SLOTS)
         w_cut(wk, 0, slot).wait()
-        depth = model // 6
-        acc[...] = jnp.zeros_like(acc)
-
-        def chunk(i, carry):
-            ks = pl.ds(pl.multiple_of(i * depth, depth), depth)
-            acc[...] += dot(normed[at, :, ks], w_buf[slot, ks, :])
-            return carry
-
-        lax.fori_loop(0, 6, chunk, 0)
-
-    def store_b(which, tile):
         cols = pl.ds(pl.multiple_of(tile * w_cols, w_cols), w_cols)
-        vals = acc[...]
-        soft = jax.nn.sigmoid(vals)
 
         @pl.when(which < 3)
         def _():
-            kvq[which, :, cols] = (vals * soft).astype(BF16)
+            for span in halves:
+                vals = dot(normed[at, span, :], w_buf[slot])
+                kvq[which, span, cols] = (vals * jax.nn.sigmoid(vals)).astype(BF16)
 
         @pl.when(which == 3)
         def _():
-            gate[:, cols] = soft
+            for span in halves:
+                gate[span, cols] = jax.nn.sigmoid(dot(normed[at, span, :], w_buf[slot]))
 
     def query_slot(batch):
         return jnp.where(batch == 3, 2, lax.rem(batch, 2))
@@ -428,32 +426,35 @@
         @pl.when(j == 2 * kv_tiles - 1)
         def _():
             kv_store(batch).start()
-            for k in range(1, n_cp):
-
-                @pl.when(c + k < n_cp)
-                def _():
-                    kv_copy(batch, k).start()
+            for mine, theirs in kv_routes:
+
+                @pl.when(c == mine)
+                def _():
+                    kv_copy(batch, theirs).start()
 
     def kv_store(batch):
         return pltpu.make_async_copy(kv_own, kv_all.at[batch, c], kv_load.at[n_cp])
 
-    def kv_copy(batch, k):
+    kv_routes = ((0, 1), (0, 2), (1, 3), (2, 3))
+    kv_relays = ((2, 0, 3), (3, 1, 2))
+
+    def kv_copy(batch, to):
         return pltpu.make_async_remote_copy(
             src_ref=kv_own,
             dst_ref=kv_all.at[batch, c],
-            send_sem=kv_send.at[k],
+            send_sem=kv_send.at[to],
             recv_sem=kv_recv.at[batch, c],
-            device_id={"cp": c + k},
+            device_id={"cp": to},
             device_id_type=MESH,
         )
 
-    def kv_arrival(batch, source):
+    def kv_relay(batch, source, to):
         return pltpu.make_async_remote_copy(
-            src_ref=kv_own,
+            src_ref=kv_all.at[batch, source],
             dst_ref=kv_all.at[batch, source],
-            send_sem=kv_send.at[0],
+            send_sem=kv_send.at[to],
             recv_sem=kv_recv.at[batch, source],
-            device_id={"cp": source},
+            device_id={"cp": to},
             device_id_type=MESH,
         )
 
@@ -462,17 +463,24 @@
 
     def load_kv(batch):
         kv_store(batch).wait()
-        for k in range(1, n_cp):
-
-            @pl.when(c + k < n_cp)
-            def _():
-                kv_copy(batch, k).wait_send()
+        for mine, theirs in kv_routes:
+
+            @pl.when(c == mine)
+            def _():
+                kv_copy(batch, theirs).wait_send()
+
+        for mine, source, theirs in kv_relays:
+
+            @pl.when(c == mine)
+            def _():
+                kv_relay(batch, source, theirs).wait_recv()
+                kv_relay(batch, source, theirs).start()
 
         for source in range(n_cp):
 
-            @pl.when(source < c)
-            def _():
-                kv_arrival(batch, source).wait_recv()
+            @pl.when((source < c) & ((c < 2) | (source != c - 2)))
+            def _():
+                kv_relay(batch, source, source).wait_recv()
 
             @pl.when(source <= c)
             def _():
@@ -483,6 +491,12 @@
             @pl.when(source <= c)
             def _():
                 kv_fetch(batch, source).wait()
+
+        for mine, source, theirs in kv_relays:
+
+            @pl.when(c == mine)
+            def _():
+                kv_relay(batch, source, theirs).wait_send()
 
     def attend(batch, pair):
         kv_head = lax.div(2 * pair, group)
@@ -548,20 +562,28 @@
         )
 
     def local_lightning():
-        def head(h, carry):
+        def one_head(h):
             cols = pl.ds(pl.multiple_of(h * HEAD, HEAD), HEAD)
             rate = slopes[h]
             key, value, query = kvq[0, :, cols], kvq[1, :, cols], kvq[2, :, cols]
-            scores = dot_t(query, key)
-            gap = lax.broadcasted_iota(jnp.int32, scores.shape, 0) - lax.broadcasted_iota(jnp.int32, scores.shape, 1)
-            decay = jnp.where(gap >= 0, jnp.exp(-rate * gap.astype(F32)), 0.0)
-            o_buf[:, cols] = dot((scores * decay).astype(BF16), value)
+            part_rows = n_tok // 3
+            for i in range(3):
+                span = slice(i * part_rows, (i + 1) * part_rows)
+                upto = slice(0, (i + 1) * part_rows)
+                scores = dot_t(query[span], key[upto])
+                gap = lax.broadcasted_iota(jnp.int32, scores.shape, 0) - lax.broadcasted_iota(jnp.int32, scores.shape, 1) + i * part_rows
+                decay = jnp.where(gap >= 0, jnp.exp(-rate * gap.astype(F32)), 0.0)
+                o_buf[span, cols] = dot((scores * decay).astype(BF16), value[upto])
             to_end = (n_tok - 1 - lax.broadcasted_iota(jnp.int32, (n_tok, HEAD), 0)).astype(F32)
             faded = key.astype(F32) * jnp.exp(-rate * to_end)
             state[h] = dot(faded.T.astype(BF16), value)
+
+        def head_pair(i, carry):
+            one_head(2 * i)
+            one_head(2 * i + 1)
             return carry
 
-        lax.fori_loop(0, n_heads, head, 0)
+        lax.fori_loop(0, n_heads // 2, head_pair, 0)
 
     def add_incoming():
         def head(h, carry):
@@ -610,20 +632,30 @@
 
         sq_acc[...] = jnp.zeros_like(sq_acc)
 
+        def cols_of(h):
+            return pl.ds(pl.multiple_of(h * HEAD, HEAD), HEAD)
+
+        def head_pair(i, carry):
+            for h in (2 * i, 2 * i + 1):
+                steps = (lax.broadcasted_iota(jnp.int32, (n_tok, HEAD), 0) + 1).astype(F32)
+                prior = dot(kvq[2, :, cols_of(h)], state_in[h].astype(BF16))
+                vals = o_buf[:, cols_of(h)] + prior * jnp.exp(-slopes[h] * steps)
+                o_buf[:, cols_of(h)] = vals
+                sq_acc[...] += vals * vals
+            return carry
+
         def head(h, carry):
-            cols = pl.ds(pl.multiple_of(h * HEAD, HEAD), HEAD)
-
-            @pl.when(c > 0)
-            def _():
-                steps = (lax.broadcasted_iota(jnp.int32, (n_tok, HEAD), 0) + 1).astype(F32)
-                prior = dot(kvq[2, :, cols], state_in[h].astype(BF16))
-                o_buf[:, cols] += prior * jnp.exp(-slopes[h] * steps)
-
-            vals = o_buf[:, cols]
+            vals = o_buf[:, cols_of(h)]
             sq_acc[...] += vals * vals
             return carry
 
-        lax.fori_loop(0, n_heads, head, 0)
+        @pl.when(c > 0)
+        def _():
+            lax.fori_loop(0, n_heads // 2, head_pair, 0)
+
+        @pl.when(c == 0)
+        def _():
+            lax.fori_loop(0, n_heads, head, 0)
 
         @pl.when((c > 0) & (batch < n_batch - 1))
         def _():
@@ -675,62 +707,84 @@
             else:
                 lax.fori_loop(0, per_group // 3, one, 0)
 
-        for at_phase, at_r, batch in ((0, 0, 1), (0, 12, 2), (1, 0, 3)):
-
-            @pl.when((phase == at_phase) & (r == at_r))
-            def _():
-                hidden_copy(batch).wait()
-
-        for at_phase, batch in ((-1, 2), (0, 3)):
-
-            @pl.when((phase == at_phase) & (r == 12))
-            def _():
-                hidden_copy(batch).start()
-
-        @pl.when(first_layer & (r == jnp.where(phase <= 0, 12, 0)))
-        def _():
-            load_kv(phase + 1)
-
-        early = phase <= 0
-        spread = 16 // n_pairs
-        first_pair = jnp.where(early, (r - 12) * (n_pairs // 4), lax.div(r, spread))
-        n_here = jnp.where(early, jnp.where(r >= 12, n_pairs // 4, 0), jnp.where(lax.rem(r, spread) == 0, 1, 0))
+        @pl.when(lax.rem(r, 4) == 0)
+        def _():
+            @pl.when(phase <= 2)
+            def _():
+                for at_phase, at_r, batch in ((0, 0, 1), (0, 20, 2), (1, 0, 3)):
+
+                    @pl.when((phase == at_phase) & (r == at_r))
+                    def _():
+                        hidden_copy(batch).wait()
+
+                for at_phase, batch in ((-1, 2), (0, 3)):
+
+                    @pl.when((phase == at_phase) & (r == 12))
+                    def _():
+                        hidden_copy(batch).start()
+
+                @pl.when(r == jnp.where(phase < 0, 12, jnp.where(phase == 0, 8, 0)))
+                def _():
+                    load_kv(phase + 1)
+
+                @pl.when(r == 8)
+                def _():
+                    for i in range(2):
+                        wo_copy(wo_a, i).start()
+
+            @pl.when(second_layer)
+            def _():
+                @pl.when((r == 4) & (c == 2))
+                def _():
+                    state_copy().wait_recv()
+                    add_incoming()
+                    send_state(phase - 3)
+
+                @pl.when(r == 8)
+                def _():
+                    for i in range(2):
+                        wo_copy(wo_l, i).start()
+
+                @pl.when(r == 12)
+                def _():
+                    add_earlier(phase - 3)
+
+                @pl.when(r == 16)
+                def _():
+                    finish_lightning(phase - 3)
+
+            @pl.when(projects)
+            def _():
+                @pl.when(r == 24)
+                def _():
+                    local_lightning()
+
+                    @pl.when(c == 0)
+                    def _():
+                        send_state(phase - 2)
+
+                @pl.when((r == 28) & (c == 1))
+                def _():
+                    state_copy().wait_recv()
+                    add_incoming()
+                    send_state(phase - 2)
 
         @pl.when(first_layer & (r < 16))
         def _():
+            later_pair = jnp.where(phase == 0, r - 8, lax.div(r, 2))
+            first_pair = jnp.where(phase < 0, (r - 12) * 2, later_pair)
+            later_here = jnp.where((phase == 0) & (r >= 8) | (phase > 0) & (lax.rem(r, 2) == 0), 1, 0)
+            n_here = jnp.where(phase < 0, jnp.where(r >= 12, 2, 0), later_here)
+
             def one_pair(i, inner):
                 attend(phase + 1, first_pair + i)
                 return inner
 
             lax.fori_loop(0, n_here, one_pair, 0)
 
-        for i in range(2):
-
-            @pl.when((r == 8 + i) & first_layer)
-            def _():
-                wo_copy(wo_a, i).start()
-
-            @pl.when((r == 8 + i) & second_layer)
-            def _():
-                wo_copy(wo_l, i).start()
-
-        @pl.when((r == 4) & second_layer & (c == 2))
-        def _():
-            state_copy().wait_recv()
-            add_incoming()
-            send_state(phase - 3)
-
-        @pl.when((r == 12) & second_layer)
-        def _():
-            add_earlier(phase - 3)
-
-        @pl.when((r == 16) & second_layer)
-        def _():
-            finish_lightning(phase - 3)
-
         wo_tile = r - 16
 
-        @pl.when((wo_tile >= 0) & (wo_tile < n_wo) & (first_layer | second_layer))
+        @pl.when((wo_tile >= 0) & (wo_tile < n_wo) & (phase < 3 + n_batch))
         def _():
             out_project(phase, wo_tile)
 
@@ -742,36 +796,19 @@
             def _():
                 wo_copy(wo_l, wo_tile + 2).start()
 
-        is_a, a_batch, a_j = a_tile(unit)
-
-        @pl.when(is_a | projects)
-        def _():
-            project(unit, jnp.where(is_a, lax.rem(a_batch, 2), lax.rem(phase, 2)))
+        @pl.when(phase <= 1)
+        def _():
+            is_a, a_batch, a_j = a_tile(unit)
 
             @pl.when(is_a)
             def _():
-                store_a(a_batch, a_j)
-
-            @pl.when(projects)
-            def _():
-                store_b(which, tile)
+                project_a(unit, a_batch, a_j)
+
+        @pl.when(projects)
+        def _():
+            project_b(unit, lax.rem(phase, 2), which, tile)
 
         fetch(unit + W_SLOTS)
-
-        @pl.when((r == 23) & projects)
-        def _():
-            local_lightning()
-
-            @pl.when(c == 0)
-            def _():
-                send_state(phase - 2)
-
-        @pl.when((r == 28) & projects & (c == 1))
-        def _():
-            state_copy().wait_recv()
-            add_incoming()
-            send_state(phase - 2)
-
         return carry
 
     hidden_copy(0).wait()
@@ -782,14 +819,36 @@
             out_copy(pieces - 4 + k, f, out).wait()
 
 
-def copy_kernel(src, dst):
-    dst[...] = src[...]
+def copy_kernel(blocks, src, dst, buf, read_sem, write_sem):
+    rows = src.shape[0] // blocks
+
+    def read(i):
+        span = pl.ds(i * rows, rows)
+        return pltpu.make_async_copy(src.at[span, :], buf.at[span, :], read_sem.at[i])
+
+    def write(i):
+        span = pl.ds(i * rows, rows)
+        return pltpu.make_async_copy(buf.at[span, :], dst.at[span, :], write_sem.at[i])
+
+    for i in range(blocks):
+        read(i).start()
+    for i in range(blocks):
+        read(i).wait()
+        write(i).start()
+    for i in range(blocks):
+        write(i).wait()
 
 
 def plain_copy(array, blocks):
-    n_rows, n_cols = array.shape
-    spec = pl.BlockSpec((n_rows // blocks, n_cols), lambda i: (i, 0))
-    return pl.pallas_call(copy_kernel, out_shape=jax.ShapeDtypeStruct(array.shape, array.dtype), grid=(blocks,), in_specs=[spec], out_specs=spec)(array)
+    shape = jax.ShapeDtypeStruct(array.shape, array.dtype)
+    return pl.pallas_call(
+        functools.partial(copy_kernel, blocks),
+        out_shape=shape,
+        in_specs=[ANY],
+        out_specs=ANY,
+        scratch_shapes=[pltpu.VMEM(array.shape, array.dtype), pltpu.SemaphoreType.DMA((blocks,)), pltpu.SemaphoreType.DMA((blocks,))],
+        compiler_params=pltpu.CompilerParams(vmem_limit_bytes=48 * 1024 * 1024),
+    )(array)
 
 
 def fused_layers(hid, weights, gains, ginner, alphas, slopes, n_tok, n_tp, n_cp):
@@ -815,7 +874,8 @@
         vmem((n_heads, HEAD, HEAD), F32),
         vmem((n_heads, HEAD, HEAD), F32),
         vmem((2, 4, rows, model), BF16),
-        vmem((rows, model), F32),
+        vmem((2, rows, model), F32),
+        vmem((2, 1, model), F32),
         vmem((n_tok, w_cols), F32),
         vmem((n_tok, HEAD), F32),
         vmem((n_tok, HEAD), F32),
@@ -852,12 +912,12 @@
             jax.ShapeDtypeStruct((n_rows, model), BF16),
             jax.ShapeDtypeStruct((n_batch, n_cp, n_tok, 2 * kv_width), BF16),
         ],
-        in_specs=[ANY] * 11 + [VMEM] * 2 + [SMEM] * 2,
+        in_specs=[ANY] * 11 + [VMEM] * 3 + [SMEM] * 2,
         out_specs=[ANY] * 3,
         scratch_shapes=scratch,
         compiler_params=pltpu.CompilerParams(collective_id=0, has_side_effects=True, vmem_limit_bytes=67043328),
         cost_estimate=pl.CostEstimate(flops=flops, bytes_accessed=12 * n_rows * model, transcendentals=0),
-    )(hid, *weights, rotary_table(n_tok * n_cp), gains, ginner, alphas, slopes)
+    )(hid, *weights, rotary_table(n_tok * n_cp), *gains, ginner, alphas, slopes)
 
 
 def solution(mesh):
@@ -866,10 +926,10 @@
     def body(hidden, alphas, wq_attn, wk_attn, wv_attn, wo_attn, gain_attn, wq_lin, wk_lin, wv_lin, wg_lin, slopes, gain_inner, wo_lin, gain_lin):
         n_batch, n_tok, model = hidden.shape
         flat = hidden.reshape(n_batch * n_tok, model)
-        gains = jnp.stack([gain_attn, gain_lin])[:, None, :]
+        gains = (gain_attn[None, :], gain_lin[None, :])
         weights = (wk_attn, wv_attn, wq_attn, wo_attn, wk_lin, wv_lin, wq_lin, wg_lin, wo_lin)
         outs = fused_layers(flat, weights, gains, gain_inner.reshape(-1, 1, HEAD), alphas, slopes, n_tok, n_tp, n_cp)
-        return plain_copy(outs[0], 12).reshape(hidden.shape)
+        return plain_copy(outs[0], 16).reshape(hidden.shape)
 
     act_spec = P("dp", "cp", None)
     rep_spec = P()

time: 1080 us -> 970 us (0.90)
  Pallas kernels: 1080 us -> 969 us
    pallas_call x1, Pallas kernels: 1060 us -> 956 us  [fused_layers(): pl.pallas_call(functools.partial(fused_kernel, n_tp, n_cp), out_shape=[ja...]
where the time goes in v3:
time: 970 us; the launch traced here: 969 us
  Pallas kernels  969 us (100%)
    pallas_call x1, Pallas kernels, fused_layers(): pl.pallas_call(functools.partial(fused_kernel, n_tp, n_cp), out_shape=[ja...  956 us

profile of v3, /device:TPU:5, one launch (start us, length us, event | category | flops | bytes accessed | tf_op | source)
XLA Modules:
  0.0 969.2 jit_solution(11345260821392252719)
XLA Ops:
  0.0 955.9 %shard_map.154 = (bf16[1536,6144]{1,0:T(8,128)(2,1)}, bf16[1536,6144]{1,0:T(8,128)(2,1)}, bf16[4,4,384,512]{3,2,1,0:T(8,128)(2,1)}) custom-call(bf16[1536,6144]{1,0:T(8,128)(2,1)} %bitcast.5, bf16[6144,256]{1,0:T(8,128)(2,1)} %wk_a.1, bf16[6144,256]{1,0:T(8,128)(2,1)} %wv_a.1, bf16[6144,2048]{1,0:T(8,128)(2,1)} %wq_a.1, bf16[2048,6144]{1,0:T(8,128)(2,1)} %wo_a.1, ...), custom_call_target="tpu_custom_call" | custom-call | flops 309237645312 | bytes 113246208 | tf_op jit(solution)/shard_map/pallas_call | solution.py:908
  955.9 13.3 %shard_map.155 = bf16[1536,6144]{1,0:T(8,128)(2,1)} custom-call(bf16[1536,6144]{1,0:T(8,128)(2,1)} %get-tuple-element.6.src), custom_call_target="tpu_custom_call" | custom-call | tf_op jit(solution)/shard_map/pallas_call | solution.py:844

commit v4 on v3

--- a/solution.py
+++ b/solution.py
@@ -137,8 +137,11 @@
     z = lax.axis_index("tp")
     c = lax.axis_index("cp")
 
+    def hidden_slot(batch):
+        return jnp.where(batch == 0, 0, 1)
+
     def hidden_copy(batch):
-        at = lax.rem(batch, 2)
+        at = hidden_slot(batch)
         return pltpu.make_async_copy(hid.at[pl.ds(pl.multiple_of(batch * n_tok, n_tok), n_tok), :], normed.at[at], hid_sem.at[at])
 
     def a_tile(unit):
@@ -146,8 +149,8 @@
         r = lax.rem(unit, UNITS)
         late = r >= 20
         j = jnp.where(late, r - 20, r)
-        is_a = (phase <= 1) & (j < a_tiles) & (jnp.logical_not(late) | (phase == 0))
-        batch = jnp.where(phase == 1, 3, jnp.where(late, 2, phase + 1))
+        is_a = (phase <= 1) & (j < a_tiles) & (jnp.logical_not(late) | (phase == 1))
+        batch = jnp.where(late, 3, phase + 1)
         return is_a, batch, j
 
     def w_cut(weight, tile, slot):
@@ -376,7 +379,7 @@
 
     def project_a(unit, batch, j):
         slot = lax.rem(unit, W_SLOTS)
-        at = lax.rem(batch, 2)
+        at = hidden_slot(batch)
         w_cut(wk, 0, slot).wait()
         for span in halves:
             acc[span, :] = dot(normed[at, span, :], w_buf[slot])
@@ -532,9 +535,14 @@
             sums[e] = jnp.zeros((n_tok, HEAD), F32)
             acc[:, e * HEAD : (e + 1) * HEAD] = jnp.zeros((n_tok, HEAD), F32)
 
+        lanes = HEAD if n_tok % HEAD == 0 else n_tok
+
         def weigh(j, carry):
             for e in range(2):
-                probs = jnp.exp2((score_refs[e][:, span(j)] - top_refs[e][:, 0:1]) * power)
+                top = top_refs[e][:, 0:lanes]
+                cuts = [pl.ds(pl.multiple_of(j * n_tok + k, lanes), lanes) for k in range(0, n_tok, lanes)]
+                parts = [jnp.exp2((score_refs[e][:, cut] - top) * power) for cut in cuts]
+                probs = jnp.concatenate(parts, axis=1) if len(parts) > 1 else parts[0]
                 sums[e] += fold(probs, jnp.add, jnp.sum, 1.0 / HEAD)
                 acc[:, e * HEAD : (e + 1) * HEAD] += dot(probs.astype(BF16), kv_buf[j, :, value_cols])
             return carry
@@ -561,7 +569,7 @@
             device_id_type=MESH,
         )
 
-    def local_lightning():
+    def local_lightning(pair):
         def one_head(h):
             cols = pl.ds(pl.multiple_of(h * HEAD, HEAD), HEAD)
             rate = slopes[h]
@@ -578,12 +586,8 @@
             faded = key.astype(F32) * jnp.exp(-rate * to_end)
             state[h] = dot(faded.T.astype(BF16), value)
 
-        def head_pair(i, carry):
-            one_head(2 * i)
-            one_head(2 * i + 1)
-            return carry
-
-        lax.fori_loop(0, n_heads // 2, head_pair, 0)
+        one_head(2 * pair)
+        one_head(2 * pair + 1)
 
     def add_incoming():
         def head(h, carry):
@@ -711,22 +715,18 @@
         def _():
             @pl.when(phase <= 2)
             def _():
-                for at_phase, at_r, batch in ((0, 0, 1), (0, 20, 2), (1, 0, 3)):
+                for at_phase, at_r, batch in ((0, 0, 1), (1, 0, 2), (1, 20, 3)):
 
                     @pl.when((phase == at_phase) & (r == at_r))
                     def _():
                         hidden_copy(batch).wait()
 
-                for at_phase, batch in ((-1, 2), (0, 3)):
+                for at_phase, batch in ((0, 2), (1, 3)):
 
                     @pl.when((phase == at_phase) & (r == 12))
                     def _():
                         hidden_copy(batch).start()
 
-                @pl.when(r == jnp.where(phase < 0, 12, jnp.where(phase == 0, 8, 0)))
-                def _():
-                    load_kv(phase + 1)
-
                 @pl.when(r == 8)
                 def _():
                     for i in range(2):
@@ -734,7 +734,7 @@
 
             @pl.when(second_layer)
             def _():
-                @pl.when((r == 4) & (c == 2))
+                @pl.when((r == 4) & (c == 1) | (r == 8) & (c == 2))
                 def _():
                     state_copy().wait_recv()
                     add_incoming()
@@ -753,60 +753,57 @@
                 def _():
                     finish_lightning(phase - 3)
 
-            @pl.when(projects)
-            def _():
-                @pl.when(r == 24)
-                def _():
-                    local_lightning()
-
-                    @pl.when(c == 0)
-                    def _():
-                        send_state(phase - 2)
-
-                @pl.when((r == 28) & (c == 1))
-                def _():
-                    state_copy().wait_recv()
-                    add_incoming()
+        @pl.when(first_layer & (r < 20))
+        def _():
+            @pl.when(r == jnp.where(phase < 0, 12, jnp.where(phase <= 1, 10, 0)))
+            def _():
+                load_kv(phase + 1)
+
+            k = r - 10
+            by_five = lax.rem(r, 5)
+            pair = jnp.where(phase < 0, 2 * (r - 12), jnp.where(phase <= 1, k - lax.div(k, 5), 2 * lax.div(r, 5) + (by_five == 2)))
+            single = (phase >= 0) & (phase <= 1) & (r >= 10) & (by_five != 4) | (phase == 2) & ((by_five == 0) | (by_five == 2))
+            n_here = jnp.where((phase < 0) & (r >= 12) & (r < 16), 2, jnp.where(single, 1, 0))
+
+            def one_pair(i, inner):
+                attend(phase + 1, pair + i)
+                return inner
+
+            lax.fori_loop(0, n_here, one_pair, 0)
+
+        wo_tile = r - jnp.where(first_layer, 20, 16)
+
+        @pl.when((wo_tile >= 0) & (wo_tile < n_wo) & (phase < 3 + n_batch))
+        def _():
+            out_project(phase, wo_tile)
+
+            @pl.when((wo_tile < n_wo - 2) & first_layer)
+            def _():
+                wo_copy(wo_a, wo_tile + 2).start()
+
+            @pl.when((wo_tile < n_wo - 2) & second_layer)
+            def _():
+                wo_copy(wo_l, wo_tile + 2).start()
+
+        @pl.when(phase <= 1)
+        def _():
+            is_a, a_batch, a_j = a_tile(unit)
+
+            @pl.when(is_a)
+            def _():
+                project_a(unit, a_batch, a_j)
+
+        @pl.when(projects)
+        def _():
+            project_b(unit, lax.rem(phase, 2), which, tile)
+
+            @pl.when(which == 3)
+            def _():
+                local_lightning(tile)
+
+                @pl.when((tile == 7) & (c == 0))
+                def _():
                     send_state(phase - 2)
-
-        @pl.when(first_layer & (r < 16))
-        def _():
-            later_pair = jnp.where(phase == 0, r - 8, lax.div(r, 2))
-            first_pair = jnp.where(phase < 0, (r - 12) * 2, later_pair)
-            later_here = jnp.where((phase == 0) & (r >= 8) | (phase > 0) & (lax.rem(r, 2) == 0), 1, 0)
-            n_here = jnp.where(phase < 0, jnp.where(r >= 12, 2, 0), later_here)
-
-            def one_pair(i, inner):
-                attend(phase + 1, first_pair + i)
-                return inner
-
-            lax.fori_loop(0, n_here, one_pair, 0)
-
-        wo_tile = r - 16
-
-        @pl.when((wo_tile >= 0) & (wo_tile < n_wo) & (phase < 3 + n_batch))
-        def _():
-            out_project(phase, wo_tile)
-
-            @pl.when((wo_tile < n_wo - 2) & first_layer)
-            def _():
-                wo_copy(wo_a, wo_tile + 2).start()
-
-            @pl.when((wo_tile < n_wo - 2) & second_layer)
-            def _():
-                wo_copy(wo_l, wo_tile + 2).start()
-
-        @pl.when(phase <= 1)
-        def _():
-            is_a, a_batch, a_j = a_tile(unit)
-
-            @pl.when(is_a)
-            def _():
-                project_a(unit, a_batch, a_j)
-
-        @pl.when(projects)
-        def _():
-            project_b(unit, lax.rem(phase, 2), which, tile)
 
         fetch(unit + W_SLOTS)
         return carry

time: 970 us -> 950 us (0.979)
  Pallas kernels: 969 us -> 949 us
    pallas_call x1, Pallas kernels: 956 us -> 936 us  [fused_layers(): pl.pallas_call(functools.partial(fused_kernel, n_tp, n_cp), out_shape=[ja...]
where the time goes in v4:
time: 950 us; the launch traced here: 949 us
  Pallas kernels  949 us (100%)
    pallas_call x1, Pallas kernels, fused_layers(): pl.pallas_call(functools.partial(fused_kernel, n_tp, n_cp), out_shape=[ja...  936 us

profile of v4, /device:TPU:5, one launch (start us, length us, event | category | flops | bytes accessed | tf_op | source)
XLA Modules:
  0.0 948.9 jit_solution(6474755866110755968)
XLA Ops:
  0.0 935.6 %shard_map.154 = (bf16[1536,6144]{1,0:T(8,128)(2,1)}, bf16[1536,6144]{1,0:T(8,128)(2,1)}, bf16[4,4,384,512]{3,2,1,0:T(8,128)(2,1)}) custom-call(bf16[1536,6144]{1,0:T(8,128)(2,1)} %bitcast.5, bf16[6144,256]{1,0:T(8,128)(2,1)} %wk_a.1, bf16[6144,256]{1,0:T(8,128)(2,1)} %wv_a.1, bf16[6144,2048]{1,0:T(8,128)(2,1)} %wq_a.1, bf16[2048,6144]{1,0:T(8,128)(2,1)} %wo_a.1, ...), custom_call_target="tpu_custom_call" | custom-call | flops 309237645312 | bytes 113246208 | tf_op jit(solution)/shard_map/pallas_call | solution.py:905
  935.6 13.3 %shard_map.155 = bf16[1536,6144]{1,0:T(8,128)(2,1)} custom-call(bf16[1536,6144]{1,0:T(8,128)(2,1)} %get-tuple-element.6.src), custom_call_target="tpu_custom_call" | custom-call | tf_op jit(solution)/shard_map/pallas_call | solution.py:841

commit v5 on v4

--- a/solution.py
+++ b/solution.py
@@ -191,10 +191,8 @@
     def has_projection(phase):
         return (phase >= 2) & (phase < 2 + n_batch)
 
-    for i in range(2):
-        hidden_copy(i).start()
-    for i in range(W_SLOTS):
-        fetch(jnp.int32(i))
+    hidden_copy(0).start()
+    fetch(jnp.int32(0))
     table_copy = pltpu.make_async_copy(table.at[pl.ds(pl.multiple_of(c * n_tok, n_tok), n_tok), :], rope.at[0], rope_sem)
     table_copy.start()
 
@@ -213,7 +211,8 @@
     rope[0] = jnp.where(lane < HEAD // 2, cosines, 1.0)
     rope[1] = jnp.where(lane < HEAD // 4, -sines, 0.0)
     rope[2] = jnp.where((lane >= HEAD // 4) & (lane < HEAD // 2), sines, 0.0)
-    pl.semaphore_wait(barrier, n_tp + n_cp - 2)
+    for i in range(1, W_SLOTS):
+        fetch(jnp.int32(i))
 
     def row_of(g, f):
         return pl.multiple_of(f * half + lax.rem(g, per_batch) * rows, rows)
@@ -464,6 +463,14 @@
     def kv_fetch(batch, source):
         return pltpu.make_async_copy(kv_all.at[batch, source], kv_buf.at[source], kv_load.at[source])
 
+    def relay_kv(batch):
+        for mine, source, theirs in kv_relays:
+
+            @pl.when(c == mine)
+            def _():
+                kv_relay(batch, source, theirs).wait_recv()
+                kv_relay(batch, source, theirs).start()
+
     def load_kv(batch):
         kv_store(batch).wait()
         for mine, theirs in kv_routes:
@@ -471,13 +478,6 @@
             @pl.when(c == mine)
             def _():
                 kv_copy(batch, theirs).wait_send()
-
-        for mine, source, theirs in kv_relays:
-
-            @pl.when(c == mine)
-            def _():
-                kv_relay(batch, source, theirs).wait_recv()
-                kv_relay(batch, source, theirs).start()
 
         for source in range(n_cp):
 
@@ -514,13 +514,18 @@
         def span(j):
             return pl.ds(pl.multiple_of(j * n_tok, n_tok), n_tok)
 
-        rows_at = lax.broadcasted_iota(jnp.int32, (n_tok, n_tok), 0)
-        keys_at = lax.broadcasted_iota(jnp.int32, (n_tok, n_tok), 1)
-        for e in range(2):
-            scores = dot_t(kvq[at, :, head_cols[e]], kv_buf[c, :, key_cols])
-            scores = jnp.where(rows_at >= keys_at, scores, -jnp.inf)
-            score_refs[e][:, span(c)] = scores
-            top_refs[e][...] = fold(scores, jnp.maximum, jnp.max, 1.0)
+        tall = n_tok // 3
+        lanes = HEAD if n_tok % HEAD == 0 else tall
+        tiles = [(slice(i * tall, (i + 1) * tall), slice(0, (i + 1) * tall), i) for i in range(3)]
+        own = [pl.ds(pl.multiple_of(c * n_tok + k, lanes), lanes) for k in range(0, n_tok, lanes)]
+        for rows_of, upto, i in tiles:
+            for e in range(2):
+                scores = dot_t(kvq[at, rows_of, head_cols[e]], kv_buf[c, upto, key_cols])
+                rows_at = lax.broadcasted_iota(jnp.int32, scores.shape, 0) + i * tall
+                scores = jnp.where(rows_at >= lax.broadcasted_iota(jnp.int32, scores.shape, 1), scores, -jnp.inf)
+                for k in range(i + 1):
+                    score_refs[e][rows_of, own[k]] = scores[:, k * tall : (k + 1) * tall]
+                top_refs[e][rows_of, :] = fold(scores, jnp.maximum, jnp.max, 1.0)
 
         def score(j, carry):
             for e in range(2):
@@ -532,10 +537,14 @@
         lax.fori_loop(0, c, score, 0)
         for e in range(2):
             top_refs[e][...] = jnp.broadcast_to(jnp.max(top_refs[e][...], axis=-1, keepdims=True), (n_tok, HEAD))
-            sums[e] = jnp.zeros((n_tok, HEAD), F32)
-            acc[:, e * HEAD : (e + 1) * HEAD] = jnp.zeros((n_tok, HEAD), F32)
-
-        lanes = HEAD if n_tok % HEAD == 0 else n_tok
+
+        for rows_of, upto, i in tiles:
+            for e in range(2):
+                top = top_refs[e][rows_of, 0:lanes]
+                parts = [jnp.exp2((score_refs[e][rows_of, own[k]] - top) * power) for k in range(i + 1)]
+                probs = jnp.concatenate(parts, axis=1) if i else parts[0]
+                sums[e, rows_of, :] = fold(probs, jnp.add, jnp.sum, 1.0 / HEAD)
+                acc[rows_of, e * HEAD : (e + 1) * HEAD] = dot(probs.astype(BF16), kv_buf[c, upto, value_cols])
 
         def weigh(j, carry):
             for e in range(2):
@@ -547,7 +556,7 @@
                 acc[:, e * HEAD : (e + 1) * HEAD] += dot(probs.astype(BF16), kv_buf[j, :, value_cols])
             return carry
 
-        lax.fori_loop(0, c + 1, weigh, 0)
+        lax.fori_loop(0, c, weigh, 0)
         for e in range(2):
             total = jnp.sum(sums[e], axis=-1, keepdims=True)
             y_buf[:, head_cols[e]] = (acc[:, e * HEAD : (e + 1) * HEAD] / total).astype(BF16)
@@ -698,6 +707,10 @@
         second_layer = (phase >= 3) & (phase < 3 + n_batch)
         projects = has_projection(phase)
 
+        @pl.when(unit == 1)
+        def _():
+            pl.semaphore_wait(barrier, n_tp + n_cp - 2)
+
         @pl.when(lax.rem(tile, 3) == 0)
         def _():
             part_of = lax.div(tile, 3)
@@ -721,9 +734,9 @@
                     def _():
                         hidden_copy(batch).wait()
 
-                for at_phase, batch in ((0, 2), (1, 3)):
-
-                    @pl.when((phase == at_phase) & (r == 12))
+                for at_phase, at_r, batch in ((-1, 4, 1), (0, 12, 2), (1, 12, 3)):
+
+                    @pl.when((phase == at_phase) & (r == at_r))
                     def _():
                         hidden_copy(batch).start()
 
@@ -755,7 +768,13 @@
 
         @pl.when(first_layer & (r < 20))
         def _():
-            @pl.when(r == jnp.where(phase < 0, 12, jnp.where(phase <= 1, 10, 0)))
+            later_start = jnp.where(phase <= 1, 10, 0)
+
+            @pl.when(r == jnp.where(phase < 0, 9, later_start))
+            def _():
+                relay_kv(phase + 1)
+
+            @pl.when(r == jnp.where(phase < 0, 12, later_start))
             def _():
                 load_kv(phase + 1)
 

time: 950 us -> 942 us (level)
  no operation moved by 1% of the time
where the time goes in v5:
time: 942 us; the launch traced here: 941 us
  Pallas kernels  941 us (100%)
    pallas_call x1, Pallas kernels, fused_layers(): pl.pallas_call(functools.partial(fused_kernel, n_tp, n_cp), out_shape=[ja...  928 us

profile of v5, /device:TPU:5, one launch (start us, length us, event | category | flops | bytes accessed | tf_op | source)
XLA Modules:
  0.0 941.4 jit_solution(18274963514170392922)
XLA Ops:
  0.0 928.0 %shard_map.154 = (bf16[1536,6144]{1,0:T(8,128)(2,1)}, bf16[1536,6144]{1,0:T(8,128)(2,1)}, bf16[4,4,384,512]{3,2,1,0:T(8,128)(2,1)}) custom-call(bf16[1536,6144]{1,0:T(8,128)(2,1)} %bitcast.5, bf16[6144,256]{1,0:T(8,128)(2,1)} %wk_a.1, bf16[6144,256]{1,0:T(8,128)(2,1)} %wv_a.1, bf16[6144,2048]{1,0:T(8,128)(2,1)} %wq_a.1, bf16[2048,6144]{1,0:T(8,128)(2,1)} %wo_a.1, ...), custom_call_target="tpu_custom_call" | custom-call | flops 309237645312 | bytes 113246208 | tf_op jit(solution)/shard_map/pallas_call | solution.py:924
  928.0 13.3 %shard_map.155 = bf16[1536,6144]{1,0:T(8,128)(2,1)} custom-call(bf16[1536,6144]{1,0:T(8,128)(2,1)} %get-tuple-element.6.src), custom_call_target="tpu_custom_call" | custom-call | tf_op jit(solution)/shard_map/pallas_call | solution.py:860
